TPU v7x, 8 devices: a whole 2x2x1 slice. The times are simulated.
8 devices in a mesh: dp: 1 (over z), cy: 2 (over y), cx: 4 (over x, core).
Axes of the slice: x: 2, y: 2, z: 1, core: 2. Of those that a mesh axis runs over, the one named last changes fastest.
Arguments:
- query_rows: bfloat16 [16384, 12, 128], P(('dp', 'cy', 'cx'))
- key_rows: bfloat16 [16384, 2, 128], P(('dp', 'cy', 'cx'))
- value_rows: bfloat16 [16384, 2, 128], P(('dp', 'cy', 'cx'))
- out_rows: bfloat16 [16384, 12, 128], P(('dp', 'cy', 'cx'))
- grad_out: bfloat16 [16384, 12, 128], P(('dp', 'cy', 'cx'))
- log_sum_exp: float32 [16384, 12], P(('dp', 'cy', 'cx'))
Outputs:
- output 1: bfloat16 [16384, 12, 128], P(('dp', 'cy', 'cx'))
- output 2: bfloat16 [16384, 2, 128], P(('dp', 'cy', 'cx'))
- output 3: bfloat16 [16384, 2, 128], P(('dp', 'cy', 'cx'))
All inputs are finite; a program needn't handle non-finite values.
Results may differ from a plain program's by a relative error of at most 0.00636.
Values are sent between devices in bfloat16 or wider.
A program may use at most 1 GiB of HBM per device.

v0:
```python
import math
import jax
import jax.numpy as jnp
from jax import lax
from jax.sharding import PartitionSpec as P


def block_grads(q_blk, do_blk, lse_blk, delta_blk, k_blk, v_blk, keep_mask, scaling):
    score_f32 = jnp.einsum('qkgd,skd->kqgs', q_blk, k_blk, preferred_element_type=jnp.float32) * scaling
    prob_f32 = jnp.exp(score_f32 - lse_blk[..., None])
    if keep_mask is not None:
        prob_f32 = jnp.where(keep_mask[None, :, None, :], prob_f32, 0.0)
    dprob_f32 = jnp.einsum('qkgd,skd->kqgs', do_blk, v_blk, preferred_element_type=jnp.float32)
    dscore_b16 = (prob_f32 * (dprob_f32 - delta_blk[..., None])).astype(jnp.bfloat16)
    prob_b16 = prob_f32.astype(jnp.bfloat16)
    dq_part = jnp.einsum('kqgs,skd->kqgd', dscore_b16, k_blk, preferred_element_type=jnp.float32)
    dk_part = jnp.einsum('kqgs,qkgd->ksd', dscore_b16, q_blk, preferred_element_type=jnp.float32)
    dv_part = jnp.einsum('kqgs,qkgd->ksd', prob_b16, do_blk, preferred_element_type=jnp.float32)
    return dq_part, dk_part, dv_part


def solution(mesh):
    n_cx = mesh.shape['cx']
    n_ctx = mesh.shape['cy'] * n_cx
    ctx_axes = ('cy', 'cx')
    shift_perm = [(dev_idx, (dev_idx + 1) % n_ctx) for dev_idx in range(n_ctx)]
    row_spec = P(('dp', 'cy', 'cx'), None, None)
    stat_spec = P(('dp', 'cy', 'cx'), None)

    def local_grads(query_rows, key_rows, value_rows, out_rows, grad_out, log_sum_exp):
        tok_dev, n_heads, head_dim = query_rows.shape
        kv_heads = key_rows.shape[1]
        group_size = n_heads // kv_heads
        half_tok = tok_dev // 2
        scaling = 1.0 / math.sqrt(head_dim)
        ctx_rank = lax.axis_index('cy') * n_cx + lax.axis_index('cx')
        q_grp = query_rows.reshape(tok_dev, kv_heads, group_size, head_dim)
        do_grp = grad_out.reshape(tok_dev, kv_heads, group_size, head_dim)
        lse_grp = log_sum_exp.reshape(tok_dev, kv_heads, group_size).transpose(1, 0, 2)
        delta_grp = jnp.einsum('thd,thd->th', grad_out, out_rows, preferred_element_type=jnp.float32).reshape(tok_dev, kv_heads, group_size).transpose(1, 0, 2)
        local_idx = jnp.arange(tok_dev)
        piece_id = jnp.where(local_idx < half_tok, ctx_rank, 2 * n_ctx - 1 - ctx_rank)
        own_pos = piece_id * half_tok + local_idx % half_tok
        diag_mask = own_pos[:, None] >= own_pos[None, :]
        dq_own, dk_own, dv_own = block_grads(q_grp, do_grp, lse_grp, delta_grp, key_rows, value_rows, diag_mask, scaling)

        def src_before(k_blk, v_blk):
            dq_part, dk_part, dv_part = block_grads(q_grp, do_grp, lse_grp, delta_grp, k_blk[:half_tok], v_blk[:half_tok], None, scaling)
            zero_pad = jnp.zeros_like(dk_part)
            return dq_part, jnp.concatenate([dk_part, zero_pad], axis=1), jnp.concatenate([dv_part, zero_pad], axis=1)

        def src_after(k_blk, v_blk):
            dq_part, dk_part, dv_part = block_grads(q_grp[half_tok:], do_grp[half_tok:], lse_grp[:, half_tok:], delta_grp[:, half_tok:], k_blk, v_blk, None, scaling)
            zero_pad = jnp.zeros_like(dq_part)
            return jnp.concatenate([zero_pad, dq_part], axis=1), dk_part, dv_part

        def step_body(step_idx, state):
            k_cur, v_cur, dk_cur, dv_cur, dq_cur = state
            k_cur = lax.ppermute(k_cur, ctx_axes, shift_perm)
            v_cur = lax.ppermute(v_cur, ctx_axes, shift_perm)
            dk_cur = lax.ppermute(dk_cur, ctx_axes, shift_perm)
            dv_cur = lax.ppermute(dv_cur, ctx_axes, shift_perm)
            src_rank = (ctx_rank - step_idx) % n_ctx
            dq_part, dk_part, dv_part = lax.cond(src_rank < ctx_rank, src_before, src_after, k_cur, v_cur)
            return (k_cur, v_cur, dk_cur + dk_part, dv_cur + dv_part, dq_cur + dq_part)

        k_end, v_end, dk_end, dv_end, dq_end = lax.fori_loop(1, n_ctx, step_body, (key_rows, value_rows, dk_own, dv_own, dq_own))
        dk_home = lax.ppermute(dk_end, ctx_axes, shift_perm)
        dv_home = lax.ppermute(dv_end, ctx_axes, shift_perm)
        grad_query = (dq_end * scaling).astype(jnp.bfloat16).transpose(1, 0, 2, 3).reshape(tok_dev, n_heads, head_dim)
        grad_key = (dk_home * scaling).astype(jnp.bfloat16).transpose(1, 0, 2)
        grad_value = dv_home.astype(jnp.bfloat16).transpose(1, 0, 2)
        return grad_query, grad_key, grad_value

    return jax.shard_map(local_grads, mesh=mesh, in_specs=(row_spec, row_spec, row_spec, row_spec, row_spec, stat_spec), out_specs=(row_spec, row_spec, row_spec), check_vma=False)
```

profile of v0, /device:TPU:0, one launch (start us, length us, event | category | flops | bytes accessed | tf_op | source)
XLA Modules:
  0.0 2409.7 jit_solution(8003252578642505994)
XLA Ops:
  16.3 67.9 %fusion.49 = f32[2,2048,6,2048]{3,1,2,0:T(8,128)} fusion(bf16[2048,2,6,128]{3,0,2,1:T(8,128)(2,1)} %bitcast.82, bf16[2048,2,128,1]{2,1,0,3:T(2,128)(2,1)S(1)} %bitcast.89), kind=kOutput, calls=%fused_computation.49 | convolution fusion | flops 12884901888 | bytes 208666624 | tf_op jit(solution)/shard_map/qkgd,skd->kqgs/dot_general | solution.py:9
  84.1 79.2 %fusion.42 = f32[2,2048,128]{2,1,0:T(8,128)} fusion(bf16[2048,2,6,128]{3,0,2,1:T(8,128)(2,1)} %bitcast.79, f32[2,2048,6,2048]{3,1,2,0:T(8,128)} %fusion.49, f32[2,2048,6]{1,2,0:T(8,128)S(1)} %bitcast.85, pred[2048,2048]{1,0:T(8,128)(4,1)} %broadcast_compare_fusion), kind=kOutput, calls=%fused_computation.41 | convolution fusion | flops 13086228480 | bytes 214007808 | tf_op jit(solution)/shard_map/kqgs,qkgd->ksd/dot_general | solution.py:18
  163.3 107.6 %multiply_convert_fusion.2 = bf16[2,2048,6,2048]{3,1,2,0:T(8,128)(2,1)} fusion(f32[2,2048,6,2048]{3,1,2,0:T(8,128)} %fusion.49, f32[2,2048,6]{1,2,0:T(8,128)} %bitcast.21, f32[2,2048,6]{1,2,0:T(8,128)S(1)} %bitcast.86, pred[2048,2048]{1,0:T(8,128)(4,1)} %broadcast_compare_fusion, bf16[2048,2,6,128]{3,0,2,1:T(8,128)(2,1)} %bitcast.80, ...), kind=kOutput, calls=%fused_computation.32 | convolution fusion | flops 13186891776 | bytes 313720832 | tf_op jit(solution)/shard_map/qkgd,skd->kqgs/dot_general | solution.py:13
  270.9 47.7 %convolution_bitcast_fusion.1 = f32[2,2048,128]{2,1,0:T(8,128)} fusion(bf16[2,2048,6,2048]{3,1,2,0:T(8,128)(2,1)} %multiply_convert_fusion.2, bf16[2048,2,6,128]{3,0,2,1:T(8,128)(2,1)} %bitcast.83), kind=kOutput, calls=%fused_computation.42 | convolution fusion | flops 12884901888 | bytes 109051904 | tf_op jit(solution)/shard_map/kqgs,qkgd->ksd/dot_general | solution.py:17
  318.6 41.3 %fusion.47 = f32[2,2048,6,128]{3,1,2,0:T(8,128)} fusion(bf16[2,2048,6,2048]{3,1,2,0:T(8,128)(2,1)} %multiply_convert_fusion.2, bf16[2048,2,128,1]{2,1,0,3:T(2,128)(2,1)S(1)} %bitcast.90), kind=kOutput, calls=%fused_computation.47 | convolution fusion | flops 12884901888 | bytes 114294784 | tf_op jit(solution)/shard_map/kqgs,skd->kqgd/dot_general | solution.py:16
  359.9 2004.6 %while.23 = (s32[]{:T(128)}, bf16[2048,2,128]{2,0,1:T(8,128)(2,1)}, bf16[2048,2,128]{2,0,1:T(8,128)(2,1)}, f32[2,2048,128]{2,1,0:T(8,128)}, f32[2,2048,128]{2,1,...) while((s32[]{:T(128)}, bf16[2048,2,128]{2,0,1:T(8,128)(2,1)}, ...), condition=%wide.region_3.4_spmd, body=%wide.region_0.3_spmd.sunk | while | flops 32417775616 | bytes 593298048 | solution.py:67
  365.2 56.1 %collective-permute-done.1 = bf16[2048,2,128]{2,0,1:T(8,128)(2,1)} collective-permute-done((bf16[2048,2,128]{2,0,1:T(8,128)(2,1)}, bf16[2048,2,128]{2,0,1:T(8,128)(2,1)}, u32[]{:S(2)}, u32[]{:S(2)}) %collective-permute-start.1) | collective-permute-done | bytes 1048608 | tf_op jit(solution)/shard_map/while/body/eval_jaxpr/ppermute | solution.py:60
  432.5 190.3 %conditional.2 = (f32[2,2048,6,128]{3,1,2,0:T(8,128)}, f32[2,2048,128]{2,1,0:T(8,128)}, f32[2,2048,128]{2,1,0:T(8,128)S(1)}) conditional(s32[]{:T(128)} %convert_element_type.65, (bf16[2048,2,6,128]{3,0,2,1:T(8,128)(2,1)}, bf16[2048,2,128]{2,0,1:T(8,128)(2,1)S(1)}, f32[2,2048,6]{1,2,0:T(8,128)S(1)}, bf16[2048,2,6,128]{3,0,2,1:T(8,128)(2,1)}, ...), branch_computations={%region_1.1_spmd, %region_2.2_spmd} | conditional | flops 32413581312 | bytes 505217088 | solution.py:64
  433.4 36.3 %fusion.7 = f32[2,1024,6,2048]{3,1,2,0:T(8,128)} fusion(bf16[2048,2,6,128]{3,0,2,1:T(8,128)(2,1)} %get-tuple-element.276, bf16[2048,2,128]{2,0,1:T(8,128)(2,1)S(1)} %get-tuple-element.277), kind=kOutput, calls=%fused_computation.8 | convolution fusion | flops 6442450944 | bytes 104857600 | tf_op jit(solution)/shard_map/while/body/eval_jaxpr/cond/branch_0_fun/qkgd,skd->kqgs/dot_general | solution.py:9
  469.7 36.4 %fusion.12 = f32[2,2048,128]{2,1,0:T(8,128)S(1)} fusion(bf16[2048,2,6,128]{3,0,2,1:T(8,128)(2,1)} %get-tuple-element.279, f32[2,1024,6,2048]{3,1,2,0:T(8,128)} %fusion.7, f32[2,1024,6]{1,2,0:T(8,128)S(1)} %slice.13), kind=kOutput, calls=%fused_computation.11 | convolution fusion | flops 6517948416 | bytes 105955328 | tf_op jit(solution)/shard_map/while/body/eval_jaxpr/cond/branch_0_fun/kqgs,qkgd->ksd/dot_general | solution.py:18
  506.1 51.2 %multiply_convert_fusion = bf16[2,1024,6,2048]{3,1,2,0:T(8,128)(2,1)} fusion(f32[2,1024,6,2048]{3,1,2,0:T(8,128)} %fusion.7, f32[2,1024,6]{1,2,0:T(8,128)S(1)} %slice.15, f32[2,1024,6]{1,2,0:T(8,128)S(1)} %slice.13, bf16[2048,2,6,128]{3,0,2,1:T(8,128)(2,1)} %get-tuple-element.279, bf16[2048,2,128]{2,0,1:T(8,128)(2,1)} %get-tuple-element.280), kind=kOutput, calls=%fused_computation | convolution fusion | flops 6568280064 | bytes 155287552 | tf_op jit(solution)/shard_map/while/body/eval_jaxpr/cond/branch_0_fun/qkgd,skd->kqgs/dot_general | solution.py:13
  557.3 26.6 %fusion.9 = f32[2,2048,128]{2,1,0:T(8,128)} fusion(bf16[2,1024,6,2048]{3,1,2,0:T(8,128)(2,1)} %multiply_convert_fusion, bf16[2048,2,6,128]{3,0,2,1:T(8,128)(2,1)} %get-tuple-element.276), kind=kOutput, calls=%fused_computation.10 | convolution fusion | flops 6442450944 | bytes 55574528 | tf_op jit(solution)/shard_map/while/body/eval_jaxpr/cond/branch_0_fun/kqgs,qkgd->ksd/dot_general | solution.py:17
  647.9 59.1 %collective-permute-done.1 = bf16[2048,2,128]{2,0,1:T(8,128)(2,1)} collective-permute-done((bf16[2048,2,128]{2,0,1:T(8,128)(2,1)}, bf16[2048,2,128]{2,0,1:T(8,128)(2,1)}, u32[]{:S(2)}, u32[]{:S(2)}) %collective-permute-start.1) | collective-permute-done | bytes 1048608 | tf_op jit(solution)/shard_map/while/body/eval_jaxpr/ppermute | solution.py:60
  718.2 190.4 %conditional.2 = (f32[2,2048,6,128]{3,1,2,0:T(8,128)}, f32[2,2048,128]{2,1,0:T(8,128)}, f32[2,2048,128]{2,1,0:T(8,128)S(1)}) conditional(s32[]{:T(128)} %convert_element_type.65, (bf16[2048,2,6,128]{3,0,2,1:T(8,128)(2,1)}, bf16[2048,2,128]{2,0,1:T(8,128)(2,1)S(1)}, f32[2,2048,6]{1,2,0:T(8,128)S(1)}, bf16[2048,2,6,128]{3,0,2,1:T(8,128)(2,1)}, ...), branch_computations={%region_1.1_spmd, %region_2.2_spmd} | conditional | flops 32413581312 | bytes 505217088 | solution.py:64
  719.1 36.3 %fusion.7 = f32[2,1024,6,2048]{3,1,2,0:T(8,128)} fusion(bf16[2048,2,6,128]{3,0,2,1:T(8,128)(2,1)} %get-tuple-element.276, bf16[2048,2,128]{2,0,1:T(8,128)(2,1)S(1)} %get-tuple-element.277), kind=kOutput, calls=%fused_computation.8 | convolution fusion | flops 6442450944 | bytes 104857600 | tf_op jit(solution)/shard_map/while/body/eval_jaxpr/cond/branch_0_fun/qkgd,skd->kqgs/dot_general | solution.py:9
  755.4 36.4 %fusion.12 = f32[2,2048,128]{2,1,0:T(8,128)S(1)} fusion(bf16[2048,2,6,128]{3,0,2,1:T(8,128)(2,1)} %get-tuple-element.279, f32[2,1024,6,2048]{3,1,2,0:T(8,128)} %fusion.7, f32[2,1024,6]{1,2,0:T(8,128)S(1)} %slice.13), kind=kOutput, calls=%fused_computation.11 | convolution fusion | flops 6517948416 | bytes 105955328 | tf_op jit(solution)/shard_map/while/body/eval_jaxpr/cond/branch_0_fun/kqgs,qkgd->ksd/dot_general | solution.py:18
  791.8 51.2 %multiply_convert_fusion = bf16[2,1024,6,2048]{3,1,2,0:T(8,128)(2,1)} fusion(f32[2,1024,6,2048]{3,1,2,0:T(8,128)} %fusion.7, f32[2,1024,6]{1,2,0:T(8,128)S(1)} %slice.15, f32[2,1024,6]{1,2,0:T(8,128)S(1)} %slice.13, bf16[2048,2,6,128]{3,0,2,1:T(8,128)(2,1)} %get-tuple-element.279, bf16[2048,2,128]{2,0,1:T(8,128)(2,1)} %get-tuple-element.280), kind=kOutput, calls=%fused_computation | convolution fusion | flops 6568280064 | bytes 155287552 | tf_op jit(solution)/shard_map/while/body/eval_jaxpr/cond/branch_0_fun/qkgd,skd->kqgs/dot_general | solution.py:13
  843.0 26.4 %fusion.9 = f32[2,2048,128]{2,1,0:T(8,128)} fusion(bf16[2,1024,6,2048]{3,1,2,0:T(8,128)(2,1)} %multiply_convert_fusion, bf16[2048,2,6,128]{3,0,2,1:T(8,128)(2,1)} %get-tuple-element.276), kind=kOutput, calls=%fused_computation.10 | convolution fusion | flops 6442450944 | bytes 55574528 | tf_op jit(solution)/shard_map/while/body/eval_jaxpr/cond/branch_0_fun/kqgs,qkgd->ksd/dot_general | solution.py:17
  932.5 59.9 %collective-permute-done.1 = bf16[2048,2,128]{2,0,1:T(8,128)(2,1)} collective-permute-done((bf16[2048,2,128]{2,0,1:T(8,128)(2,1)}, bf16[2048,2,128]{2,0,1:T(8,128)(2,1)}, u32[]{:S(2)}, u32[]{:S(2)}) %collective-permute-start.1) | collective-permute-done | bytes 1048608 | tf_op jit(solution)/shard_map/while/body/eval_jaxpr/ppermute | solution.py:60
  1003.6 190.3 %conditional.2 = (f32[2,2048,6,128]{3,1,2,0:T(8,128)}, f32[2,2048,128]{2,1,0:T(8,128)}, f32[2,2048,128]{2,1,0:T(8,128)S(1)}) conditional(s32[]{:T(128)} %convert_element_type.65, (bf16[2048,2,6,128]{3,0,2,1:T(8,128)(2,1)}, bf16[2048,2,128]{2,0,1:T(8,128)(2,1)S(1)}, f32[2,2048,6]{1,2,0:T(8,128)S(1)}, bf16[2048,2,6,128]{3,0,2,1:T(8,128)(2,1)}, ...), branch_computations={%region_1.1_spmd, %region_2.2_spmd} | conditional | flops 32413581312 | bytes 505217088 | solution.py:64
  1004.5 36.3 %fusion.7 = f32[2,1024,6,2048]{3,1,2,0:T(8,128)} fusion(bf16[2048,2,6,128]{3,0,2,1:T(8,128)(2,1)} %get-tuple-element.276, bf16[2048,2,128]{2,0,1:T(8,128)(2,1)S(1)} %get-tuple-element.277), kind=kOutput, calls=%fused_computation.8 | convolution fusion | flops 6442450944 | bytes 104857600 | tf_op jit(solution)/shard_map/while/body/eval_jaxpr/cond/branch_0_fun/qkgd,skd->kqgs/dot_general | solution.py:9
  1040.8 36.4 %fusion.12 = f32[2,2048,128]{2,1,0:T(8,128)S(1)} fusion(bf16[2048,2,6,128]{3,0,2,1:T(8,128)(2,1)} %get-tuple-element.279, f32[2,1024,6,2048]{3,1,2,0:T(8,128)} %fusion.7, f32[2,1024,6]{1,2,0:T(8,128)S(1)} %slice.13), kind=kOutput, calls=%fused_computation.11 | convolution fusion | flops 6517948416 | bytes 105955328 | tf_op jit(solution)/shard_map/while/body/eval_jaxpr/cond/branch_0_fun/kqgs,qkgd->ksd/dot_general | solution.py:18
  1077.2 51.2 %multiply_convert_fusion = bf16[2,1024,6,2048]{3,1,2,0:T(8,128)(2,1)} fusion(f32[2,1024,6,2048]{3,1,2,0:T(8,128)} %fusion.7, f32[2,1024,6]{1,2,0:T(8,128)S(1)} %slice.15, f32[2,1024,6]{1,2,0:T(8,128)S(1)} %slice.13, bf16[2048,2,6,128]{3,0,2,1:T(8,128)(2,1)} %get-tuple-element.279, bf16[2048,2,128]{2,0,1:T(8,128)(2,1)} %get-tuple-element.280), kind=kOutput, calls=%fused_computation | convolution fusion | flops 6568280064 | bytes 155287552 | tf_op jit(solution)/shard_map/while/body/eval_jaxpr/cond/branch_0_fun/qkgd,skd->kqgs/dot_general | solution.py:13
  1128.4 26.4 %fusion.9 = f32[2,2048,128]{2,1,0:T(8,128)} fusion(bf16[2,1024,6,2048]{3,1,2,0:T(8,128)(2,1)} %multiply_convert_fusion, bf16[2048,2,6,128]{3,0,2,1:T(8,128)(2,1)} %get-tuple-element.276), kind=kOutput, calls=%fused_computation.10 | convolution fusion | flops 6442450944 | bytes 55574528 | tf_op jit(solution)/shard_map/while/body/eval_jaxpr/cond/branch_0_fun/kqgs,qkgd->ksd/dot_general | solution.py:17
  1218.0 59.9 %collective-permute-done.1 = bf16[2048,2,128]{2,0,1:T(8,128)(2,1)} collective-permute-done((bf16[2048,2,128]{2,0,1:T(8,128)(2,1)}, bf16[2048,2,128]{2,0,1:T(8,128)(2,1)}, u32[]{:S(2)}, u32[]{:S(2)}) %collective-permute-start.1) | collective-permute-done | bytes 1048608 | tf_op jit(solution)/shard_map/while/body/eval_jaxpr/ppermute | solution.py:60
  1289.1 190.4 %conditional.2 = (f32[2,2048,6,128]{3,1,2,0:T(8,128)}, f32[2,2048,128]{2,1,0:T(8,128)}, f32[2,2048,128]{2,1,0:T(8,128)S(1)}) conditional(s32[]{:T(128)} %convert_element_type.65, (bf16[2048,2,6,128]{3,0,2,1:T(8,128)(2,1)}, bf16[2048,2,128]{2,0,1:T(8,128)(2,1)S(1)}, f32[2,2048,6]{1,2,0:T(8,128)S(1)}, bf16[2048,2,6,128]{3,0,2,1:T(8,128)(2,1)}, ...), branch_computations={%region_1.1_spmd, %region_2.2_spmd} | conditional | flops 32413581312 | bytes 505217088 | solution.py:64
  1290.0 36.3 %fusion.7 = f32[2,1024,6,2048]{3,1,2,0:T(8,128)} fusion(bf16[2048,2,6,128]{3,0,2,1:T(8,128)(2,1)} %get-tuple-element.276, bf16[2048,2,128]{2,0,1:T(8,128)(2,1)S(1)} %get-tuple-element.277), kind=kOutput, calls=%fused_computation.8 | convolution fusion | flops 6442450944 | bytes 104857600 | tf_op jit(solution)/shard_map/while/body/eval_jaxpr/cond/branch_0_fun/qkgd,skd->kqgs/dot_general | solution.py:9
  1326.3 36.4 %fusion.12 = f32[2,2048,128]{2,1,0:T(8,128)S(1)} fusion(bf16[2048,2,6,128]{3,0,2,1:T(8,128)(2,1)} %get-tuple-element.279, f32[2,1024,6,2048]{3,1,2,0:T(8,128)} %fusion.7, f32[2,1024,6]{1,2,0:T(8,128)S(1)} %slice.13), kind=kOutput, calls=%fused_computation.11 | convolution fusion | flops 6517948416 | bytes 105955328 | tf_op jit(solution)/shard_map/while/body/eval_jaxpr/cond/branch_0_fun/kqgs,qkgd->ksd/dot_general | solution.py:18
  1362.7 51.2 %multiply_convert_fusion = bf16[2,1024,6,2048]{3,1,2,0:T(8,128)(2,1)} fusion(f32[2,1024,6,2048]{3,1,2,0:T(8,128)} %fusion.7, f32[2,1024,6]{1,2,0:T(8,128)S(1)} %slice.15, f32[2,1024,6]{1,2,0:T(8,128)S(1)} %slice.13, bf16[2048,2,6,128]{3,0,2,1:T(8,128)(2,1)} %get-tuple-element.279, bf16[2048,2,128]{2,0,1:T(8,128)(2,1)} %get-tuple-element.280), kind=kOutput, calls=%fused_computation | convolution fusion | flops 6568280064 | bytes 155287552 | tf_op jit(solution)/shard_map/while/body/eval_jaxpr/cond/branch_0_fun/qkgd,skd->kqgs/dot_general | solution.py:13
  1413.9 26.7 %fusion.9 = f32[2,2048,128]{2,1,0:T(8,128)} fusion(bf16[2,1024,6,2048]{3,1,2,0:T(8,128)(2,1)} %multiply_convert_fusion, bf16[2048,2,6,128]{3,0,2,1:T(8,128)(2,1)} %get-tuple-element.276), kind=kOutput, calls=%fused_computation.10 | convolution fusion | flops 6442450944 | bytes 55574528 | tf_op jit(solution)/shard_map/while/body/eval_jaxpr/cond/branch_0_fun/kqgs,qkgd->ksd/dot_general | solution.py:17
  1503.7 59.9 %collective-permute-done.1 = bf16[2048,2,128]{2,0,1:T(8,128)(2,1)} collective-permute-done((bf16[2048,2,128]{2,0,1:T(8,128)(2,1)}, bf16[2048,2,128]{2,0,1:T(8,128)(2,1)}, u32[]{:S(2)}, u32[]{:S(2)}) %collective-permute-start.1) | collective-permute-done | bytes 1048608 | tf_op jit(solution)/shard_map/while/body/eval_jaxpr/ppermute | solution.py:60
  1574.9 190.4 %conditional.2 = (f32[2,2048,6,128]{3,1,2,0:T(8,128)}, f32[2,2048,128]{2,1,0:T(8,128)}, f32[2,2048,128]{2,1,0:T(8,128)S(1)}) conditional(s32[]{:T(128)} %convert_element_type.65, (bf16[2048,2,6,128]{3,0,2,1:T(8,128)(2,1)}, bf16[2048,2,128]{2,0,1:T(8,128)(2,1)S(1)}, f32[2,2048,6]{1,2,0:T(8,128)S(1)}, bf16[2048,2,6,128]{3,0,2,1:T(8,128)(2,1)}, ...), branch_computations={%region_1.1_spmd, %region_2.2_spmd} | conditional | flops 32413581312 | bytes 505217088 | solution.py:64
  1575.7 36.3 %fusion.7 = f32[2,1024,6,2048]{3,1,2,0:T(8,128)} fusion(bf16[2048,2,6,128]{3,0,2,1:T(8,128)(2,1)} %get-tuple-element.276, bf16[2048,2,128]{2,0,1:T(8,128)(2,1)S(1)} %get-tuple-element.277), kind=kOutput, calls=%fused_computation.8 | convolution fusion | flops 6442450944 | bytes 104857600 | tf_op jit(solution)/shard_map/while/body/eval_jaxpr/cond/branch_0_fun/qkgd,skd->kqgs/dot_general | solution.py:9
  1612.1 36.4 %fusion.12 = f32[2,2048,128]{2,1,0:T(8,128)S(1)} fusion(bf16[2048,2,6,128]{3,0,2,1:T(8,128)(2,1)} %get-tuple-element.279, f32[2,1024,6,2048]{3,1,2,0:T(8,128)} %fusion.7, f32[2,1024,6]{1,2,0:T(8,128)S(1)} %slice.13), kind=kOutput, calls=%fused_computation.11 | convolution fusion | flops 6517948416 | bytes 105955328 | tf_op jit(solution)/shard_map/while/body/eval_jaxpr/cond/branch_0_fun/kqgs,qkgd->ksd/dot_general | solution.py:18
  1648.5 51.2 %multiply_convert_fusion = bf16[2,1024,6,2048]{3,1,2,0:T(8,128)(2,1)} fusion(f32[2,1024,6,2048]{3,1,2,0:T(8,128)} %fusion.7, f32[2,1024,6]{1,2,0:T(8,128)S(1)} %slice.15, f32[2,1024,6]{1,2,0:T(8,128)S(1)} %slice.13, bf16[2048,2,6,128]{3,0,2,1:T(8,128)(2,1)} %get-tuple-element.279, bf16[2048,2,128]{2,0,1:T(8,128)(2,1)} %get-tuple-element.280), kind=kOutput, calls=%fused_computation | convolution fusion | flops 6568280064 | bytes 155287552 | tf_op jit(solution)/shard_map/while/body/eval_jaxpr/cond/branch_0_fun/qkgd,skd->kqgs/dot_general | solution.py:13
  1699.7 26.4 %fusion.9 = f32[2,2048,128]{2,1,0:T(8,128)} fusion(bf16[2,1024,6,2048]{3,1,2,0:T(8,128)(2,1)} %multiply_convert_fusion, bf16[2048,2,6,128]{3,0,2,1:T(8,128)(2,1)} %get-tuple-element.276), kind=kOutput, calls=%fused_computation.10 | convolution fusion | flops 6442450944 | bytes 55574528 | tf_op jit(solution)/shard_map/while/body/eval_jaxpr/cond/branch_0_fun/kqgs,qkgd->ksd/dot_general | solution.py:17
  1789.2 59.9 %collective-permute-done.1 = bf16[2048,2,128]{2,0,1:T(8,128)(2,1)} collective-permute-done((bf16[2048,2,128]{2,0,1:T(8,128)(2,1)}, bf16[2048,2,128]{2,0,1:T(8,128)(2,1)}, u32[]{:S(2)}, u32[]{:S(2)}) %collective-permute-start.1) | collective-permute-done | bytes 1048608 | tf_op jit(solution)/shard_map/while/body/eval_jaxpr/ppermute | solution.py:60
  1860.3 190.3 %conditional.2 = (f32[2,2048,6,128]{3,1,2,0:T(8,128)}, f32[2,2048,128]{2,1,0:T(8,128)}, f32[2,2048,128]{2,1,0:T(8,128)S(1)}) conditional(s32[]{:T(128)} %convert_element_type.65, (bf16[2048,2,6,128]{3,0,2,1:T(8,128)(2,1)}, bf16[2048,2,128]{2,0,1:T(8,128)(2,1)S(1)}, f32[2,2048,6]{1,2,0:T(8,128)S(1)}, bf16[2048,2,6,128]{3,0,2,1:T(8,128)(2,1)}, ...), branch_computations={%region_1.1_spmd, %region_2.2_spmd} | conditional | flops 32413581312 | bytes 505217088 | solution.py:64
  1861.2 36.3 %fusion.7 = f32[2,1024,6,2048]{3,1,2,0:T(8,128)} fusion(bf16[2048,2,6,128]{3,0,2,1:T(8,128)(2,1)} %get-tuple-element.276, bf16[2048,2,128]{2,0,1:T(8,128)(2,1)S(1)} %get-tuple-element.277), kind=kOutput, calls=%fused_computation.8 | convolution fusion | flops 6442450944 | bytes 104857600 | tf_op jit(solution)/shard_map/while/body/eval_jaxpr/cond/branch_0_fun/qkgd,skd->kqgs/dot_general | solution.py:9
  1897.5 36.4 %fusion.12 = f32[2,2048,128]{2,1,0:T(8,128)S(1)} fusion(bf16[2048,2,6,128]{3,0,2,1:T(8,128)(2,1)} %get-tuple-element.279, f32[2,1024,6,2048]{3,1,2,0:T(8,128)} %fusion.7, f32[2,1024,6]{1,2,0:T(8,128)S(1)} %slice.13), kind=kOutput, calls=%fused_computation.11 | convolution fusion | flops 6517948416 | bytes 105955328 | tf_op jit(solution)/shard_map/while/body/eval_jaxpr/cond/branch_0_fun/kqgs,qkgd->ksd/dot_general | solution.py:18
  1933.9 51.2 %multiply_convert_fusion = bf16[2,1024,6,2048]{3,1,2,0:T(8,128)(2,1)} fusion(f32[2,1024,6,2048]{3,1,2,0:T(8,128)} %fusion.7, f32[2,1024,6]{1,2,0:T(8,128)S(1)} %slice.15, f32[2,1024,6]{1,2,0:T(8,128)S(1)} %slice.13, bf16[2048,2,6,128]{3,0,2,1:T(8,128)(2,1)} %get-tuple-element.279, bf16[2048,2,128]{2,0,1:T(8,128)(2,1)} %get-tuple-element.280), kind=kOutput, calls=%fused_computation | convolution fusion | flops 6568280064 | bytes 155287552 | tf_op jit(solution)/shard_map/while/body/eval_jaxpr/cond/branch_0_fun/qkgd,skd->kqgs/dot_general | solution.py:13
  1985.1 26.4 %fusion.9 = f32[2,2048,128]{2,1,0:T(8,128)} fusion(bf16[2,1024,6,2048]{3,1,2,0:T(8,128)(2,1)} %multiply_convert_fusion, bf16[2048,2,6,128]{3,0,2,1:T(8,128)(2,1)} %get-tuple-element.276), kind=kOutput, calls=%fused_computation.10 | convolution fusion | flops 6442450944 | bytes 55574528 | tf_op jit(solution)/shard_map/while/body/eval_jaxpr/cond/branch_0_fun/kqgs,qkgd->ksd/dot_general | solution.py:17
  2074.7 59.9 %collective-permute-done.1 = bf16[2048,2,128]{2,0,1:T(8,128)(2,1)} collective-permute-done((bf16[2048,2,128]{2,0,1:T(8,128)(2,1)}, bf16[2048,2,128]{2,0,1:T(8,128)(2,1)}, u32[]{:S(2)}, u32[]{:S(2)}) %collective-permute-start.1) | collective-permute-done | bytes 1048608 | tf_op jit(solution)/shard_map/while/body/eval_jaxpr/ppermute | solution.py:60
  2145.8 190.4 %conditional.2 = (f32[2,2048,6,128]{3,1,2,0:T(8,128)}, f32[2,2048,128]{2,1,0:T(8,128)}, f32[2,2048,128]{2,1,0:T(8,128)S(1)}) conditional(s32[]{:T(128)} %convert_element_type.65, (bf16[2048,2,6,128]{3,0,2,1:T(8,128)(2,1)}, bf16[2048,2,128]{2,0,1:T(8,128)(2,1)S(1)}, f32[2,2048,6]{1,2,0:T(8,128)S(1)}, bf16[2048,2,6,128]{3,0,2,1:T(8,128)(2,1)}, ...), branch_computations={%region_1.1_spmd, %region_2.2_spmd} | conditional | flops 32413581312 | bytes 505217088 | solution.py:64
  2146.7 36.3 %fusion.7 = f32[2,1024,6,2048]{3,1,2,0:T(8,128)} fusion(bf16[2048,2,6,128]{3,0,2,1:T(8,128)(2,1)} %get-tuple-element.276, bf16[2048,2,128]{2,0,1:T(8,128)(2,1)S(1)} %get-tuple-element.277), kind=kOutput, calls=%fused_computation.8 | convolution fusion | flops 6442450944 | bytes 104857600 | tf_op jit(solution)/shard_map/while/body/eval_jaxpr/cond/branch_0_fun/qkgd,skd->kqgs/dot_general | solution.py:9
  2183.0 36.4 %fusion.12 = f32[2,2048,128]{2,1,0:T(8,128)S(1)} fusion(bf16[2048,2,6,128]{3,0,2,1:T(8,128)(2,1)} %get-tuple-element.279, f32[2,1024,6,2048]{3,1,2,0:T(8,128)} %fusion.7, f32[2,1024,6]{1,2,0:T(8,128)S(1)} %slice.13), kind=kOutput, calls=%fused_computation.11 | convolution fusion | flops 6517948416 | bytes 105955328 | tf_op jit(solution)/shard_map/while/body/eval_jaxpr/cond/branch_0_fun/kqgs,qkgd->ksd/dot_general | solution.py:18
  2219.4 51.2 %multiply_convert_fusion = bf16[2,1024,6,2048]{3,1,2,0:T(8,128)(2,1)} fusion(f32[2,1024,6,2048]{3,1,2,0:T(8,128)} %fusion.7, f32[2,1024,6]{1,2,0:T(8,128)S(1)} %slice.15, f32[2,1024,6]{1,2,0:T(8,128)S(1)} %slice.13, bf16[2048,2,6,128]{3,0,2,1:T(8,128)(2,1)} %get-tuple-element.279, bf16[2048,2,128]{2,0,1:T(8,128)(2,1)} %get-tuple-element.280), kind=kOutput, calls=%fused_computation | convolution fusion | flops 6568280064 | bytes 155287552 | tf_op jit(solution)/shard_map/while/body/eval_jaxpr/cond/branch_0_fun/qkgd,skd->kqgs/dot_general | solution.py:13
  2270.6 26.7 %fusion.9 = f32[2,2048,128]{2,1,0:T(8,128)} fusion(bf16[2,1024,6,2048]{3,1,2,0:T(8,128)(2,1)} %multiply_convert_fusion, bf16[2048,2,6,128]{3,0,2,1:T(8,128)(2,1)} %get-tuple-element.276), kind=kOutput, calls=%fused_computation.10 | convolution fusion | flops 6442450944 | bytes 55574528 | tf_op jit(solution)/shard_map/while/body/eval_jaxpr/cond/branch_0_fun/kqgs,qkgd->ksd/dot_general | solution.py:17
  (150 shorter events, 534.4 us)
Async XLA Ops:
  0.6 8.8 copy-start.5
  0.6 8.8 copy-start.2
  0.7 9.9 copy-start.4
  270.9 47.7 %copy-start.3 = (bf16[2048,2,128]{2,1,0:T(2,128)(2,1)S(1)}, bf16[2048,2,128]{2,1,0:T(2,128)(2,1)}, u32[]{:S(2)}) copy-start(bf16[2048,2,128]{2,1,0:T(2,128)(2,1)} %param.11) | copy-start | bytes 3145732
  360.1 280.0 %collective-permute-start.2 = (f32[2,2048,128]{2,1,0:T(8,128)}, f32[2,2048,128]{2,1,0:T(8,128)}, u32[]{:S(2)}, u32[]{:S(2)}) collective-permute-start(f32[2,2048,128]{2,1,0:T(8,128)} %get-tuple-element.453), channel_id=1, source_target_pairs={{0,1},{1,2},{2,3},{3,4},{4,5},{5,6},{6,7},{7,0}} | collective-permute-start | bytes 6291464 | tf_op jit(solution)/shard_map/while/body/eval_jaxpr/ppermute | solution.py:61
  361.0 282.3 %collective-permute-start.3 = (f32[2,2048,128]{2,1,0:T(8,128)}, f32[2,2048,128]{2,1,0:T(8,128)}, u32[]{:S(2)}, u32[]{:S(2)}) collective-permute-start(f32[2,2048,128]{2,1,0:T(8,128)} %get-tuple-element.454), channel_id=1, source_target_pairs={{0,1},{1,2},{2,3},{3,4},{4,5},{5,6},{6,7},{7,0}} | collective-permute-start | bytes 6291464 | tf_op jit(solution)/shard_map/while/body/eval_jaxpr/ppermute | solution.py:62
  363.6 57.7 %collective-permute-start.1 = (bf16[2048,2,128]{2,0,1:T(8,128)(2,1)}, bf16[2048,2,128]{2,0,1:T(8,128)(2,1)}, u32[]{:S(2)}, u32[]{:S(2)}) collective-permute-start(bf16[2048,2,128]{2,0,1:T(8,128)(2,1)} %get-tuple-element.452), channel_id=1, source_target_pairs={{0,1},{1,2},{2,3},{3,4},{4,5},{5,6},{6,7},{7,0}} | collective-permute-start | bytes 3145736 | tf_op jit(solution)/shard_map/while/body/eval_jaxpr/ppermute | solution.py:60
  363.6 68.9 %collective-permute-start = (bf16[2048,2,128]{2,0,1:T(8,128)(2,1)}, bf16[2048,2,128]{2,0,1:T(8,128)(2,1)S(1)}, u32[]{:S(2)}, u32[]{:S(2)}) collective-permute-start(bf16[2048,2,128]{2,0,1:T(8,128)(2,1)} %get-tuple-element.451), channel_id=1, source_target_pairs={{0,1},{1,2},{2,3},{3,4},{4,5},{5,6},{6,7},{7,0}} | collective-permute-start | bytes 3145736 | tf_op jit(solution)/shard_map/while/body/eval_jaxpr/ppermute | solution.py:59
  622.9 17.3 copy-start
  646.9 279.0 %collective-permute-start.2 = (f32[2,2048,128]{2,1,0:T(8,128)}, f32[2,2048,128]{2,1,0:T(8,128)}, u32[]{:S(2)}, u32[]{:S(2)}) collective-permute-start(f32[2,2048,128]{2,1,0:T(8,128)} %get-tuple-element.453), channel_id=1, source_target_pairs={{0,1},{1,2},{2,3},{3,4},{4,5},{5,6},{6,7},{7,0}} | collective-permute-start | bytes 6291464 | tf_op jit(solution)/shard_map/while/body/eval_jaxpr/ppermute | solution.py:61
  646.9 282.1 %collective-permute-start.3 = (f32[2,2048,128]{2,1,0:T(8,128)}, f32[2,2048,128]{2,1,0:T(8,128)}, u32[]{:S(2)}, u32[]{:S(2)}) collective-permute-start(f32[2,2048,128]{2,1,0:T(8,128)} %get-tuple-element.454), channel_id=1, source_target_pairs={{0,1},{1,2},{2,3},{3,4},{4,5},{5,6},{6,7},{7,0}} | collective-permute-start | bytes 6291464 | tf_op jit(solution)/shard_map/while/body/eval_jaxpr/ppermute | solution.py:62
  647.0 60.0 %collective-permute-start.1 = (bf16[2048,2,128]{2,0,1:T(8,128)(2,1)}, bf16[2048,2,128]{2,0,1:T(8,128)(2,1)}, u32[]{:S(2)}, u32[]{:S(2)}) collective-permute-start(bf16[2048,2,128]{2,0,1:T(8,128)(2,1)} %get-tuple-element.452), channel_id=1, source_target_pairs={{0,1},{1,2},{2,3},{3,4},{4,5},{5,6},{6,7},{7,0}} | collective-permute-start | bytes 3145736 | tf_op jit(solution)/shard_map/while/body/eval_jaxpr/ppermute | solution.py:60
  647.0 71.2 %collective-permute-start = (bf16[2048,2,128]{2,0,1:T(8,128)(2,1)}, bf16[2048,2,128]{2,0,1:T(8,128)(2,1)S(1)}, u32[]{:S(2)}, u32[]{:S(2)}) collective-permute-start(bf16[2048,2,128]{2,0,1:T(8,128)(2,1)} %get-tuple-element.451), channel_id=1, source_target_pairs={{0,1},{1,2},{2,3},{3,4},{4,5},{5,6},{6,7},{7,0}} | collective-permute-start | bytes 3145736 | tf_op jit(solution)/shard_map/while/body/eval_jaxpr/ppermute | solution.py:59
  908.6 17.3 copy-start
  932.3 278.9 %collective-permute-start.2 = (f32[2,2048,128]{2,1,0:T(8,128)}, f32[2,2048,128]{2,1,0:T(8,128)}, u32[]{:S(2)}, u32[]{:S(2)}) collective-permute-start(f32[2,2048,128]{2,1,0:T(8,128)} %get-tuple-element.453), channel_id=1, source_target_pairs={{0,1},{1,2},{2,3},{3,4},{4,5},{5,6},{6,7},{7,0}} | collective-permute-start | bytes 6291464 | tf_op jit(solution)/shard_map/while/body/eval_jaxpr/ppermute | solution.py:61
  932.4 282.1 %collective-permute-start.3 = (f32[2,2048,128]{2,1,0:T(8,128)}, f32[2,2048,128]{2,1,0:T(8,128)}, u32[]{:S(2)}, u32[]{:S(2)}) collective-permute-start(f32[2,2048,128]{2,1,0:T(8,128)} %get-tuple-element.454), channel_id=1, source_target_pairs={{0,1},{1,2},{2,3},{3,4},{4,5},{5,6},{6,7},{7,0}} | collective-permute-start | bytes 6291464 | tf_op jit(solution)/shard_map/while/body/eval_jaxpr/ppermute | solution.py:62
  932.4 60.0 %collective-permute-start.1 = (bf16[2048,2,128]{2,0,1:T(8,128)(2,1)}, bf16[2048,2,128]{2,0,1:T(8,128)(2,1)}, u32[]{:S(2)}, u32[]{:S(2)}) collective-permute-start(bf16[2048,2,128]{2,0,1:T(8,128)(2,1)} %get-tuple-element.452), channel_id=1, source_target_pairs={{0,1},{1,2},{2,3},{3,4},{4,5},{5,6},{6,7},{7,0}} | collective-permute-start | bytes 3145736 | tf_op jit(solution)/shard_map/while/body/eval_jaxpr/ppermute | solution.py:60
  932.4 71.2 %collective-permute-start = (bf16[2048,2,128]{2,0,1:T(8,128)(2,1)}, bf16[2048,2,128]{2,0,1:T(8,128)(2,1)S(1)}, u32[]{:S(2)}, u32[]{:S(2)}) collective-permute-start(bf16[2048,2,128]{2,0,1:T(8,128)(2,1)} %get-tuple-element.451), channel_id=1, source_target_pairs={{0,1},{1,2},{2,3},{3,4},{4,5},{5,6},{6,7},{7,0}} | collective-permute-start | bytes 3145736 | tf_op jit(solution)/shard_map/while/body/eval_jaxpr/ppermute | solution.py:59
  1194.0 17.3 copy-start
  1217.8 279.0 %collective-permute-start.2 = (f32[2,2048,128]{2,1,0:T(8,128)}, f32[2,2048,128]{2,1,0:T(8,128)}, u32[]{:S(2)}, u32[]{:S(2)}) collective-permute-start(f32[2,2048,128]{2,1,0:T(8,128)} %get-tuple-element.453), channel_id=1, source_target_pairs={{0,1},{1,2},{2,3},{3,4},{4,5},{5,6},{6,7},{7,0}} | collective-permute-start | bytes 6291464 | tf_op jit(solution)/shard_map/while/body/eval_jaxpr/ppermute | solution.py:61
  1217.8 282.1 %collective-permute-start.3 = (f32[2,2048,128]{2,1,0:T(8,128)}, f32[2,2048,128]{2,1,0:T(8,128)}, u32[]{:S(2)}, u32[]{:S(2)}) collective-permute-start(f32[2,2048,128]{2,1,0:T(8,128)} %get-tuple-element.454), channel_id=1, source_target_pairs={{0,1},{1,2},{2,3},{3,4},{4,5},{5,6},{6,7},{7,0}} | collective-permute-start | bytes 6291464 | tf_op jit(solution)/shard_map/while/body/eval_jaxpr/ppermute | solution.py:62
  1217.9 60.0 %collective-permute-start.1 = (bf16[2048,2,128]{2,0,1:T(8,128)(2,1)}, bf16[2048,2,128]{2,0,1:T(8,128)(2,1)}, u32[]{:S(2)}, u32[]{:S(2)}) collective-permute-start(bf16[2048,2,128]{2,0,1:T(8,128)(2,1)} %get-tuple-element.452), channel_id=1, source_target_pairs={{0,1},{1,2},{2,3},{3,4},{4,5},{5,6},{6,7},{7,0}} | collective-permute-start | bytes 3145736 | tf_op jit(solution)/shard_map/while/body/eval_jaxpr/ppermute | solution.py:60
  1217.9 71.2 %collective-permute-start = (bf16[2048,2,128]{2,0,1:T(8,128)(2,1)}, bf16[2048,2,128]{2,0,1:T(8,128)(2,1)S(1)}, u32[]{:S(2)}, u32[]{:S(2)}) collective-permute-start(bf16[2048,2,128]{2,0,1:T(8,128)(2,1)} %get-tuple-element.451), channel_id=1, source_target_pairs={{0,1},{1,2},{2,3},{3,4},{4,5},{5,6},{6,7},{7,0}} | collective-permute-start | bytes 3145736 | tf_op jit(solution)/shard_map/while/body/eval_jaxpr/ppermute | solution.py:59
  1479.5 17.3 copy-start
  1503.6 279.0 %collective-permute-start.2 = (f32[2,2048,128]{2,1,0:T(8,128)}, f32[2,2048,128]{2,1,0:T(8,128)}, u32[]{:S(2)}, u32[]{:S(2)}) collective-permute-start(f32[2,2048,128]{2,1,0:T(8,128)} %get-tuple-element.453), channel_id=1, source_target_pairs={{0,1},{1,2},{2,3},{3,4},{4,5},{5,6},{6,7},{7,0}} | collective-permute-start | bytes 6291464 | tf_op jit(solution)/shard_map/while/body/eval_jaxpr/ppermute | solution.py:61
  1503.6 282.1 %collective-permute-start.3 = (f32[2,2048,128]{2,1,0:T(8,128)}, f32[2,2048,128]{2,1,0:T(8,128)}, u32[]{:S(2)}, u32[]{:S(2)}) collective-permute-start(f32[2,2048,128]{2,1,0:T(8,128)} %get-tuple-element.454), channel_id=1, source_target_pairs={{0,1},{1,2},{2,3},{3,4},{4,5},{5,6},{6,7},{7,0}} | collective-permute-start | bytes 6291464 | tf_op jit(solution)/shard_map/while/body/eval_jaxpr/ppermute | solution.py:62
  1503.6 60.0 %collective-permute-start.1 = (bf16[2048,2,128]{2,0,1:T(8,128)(2,1)}, bf16[2048,2,128]{2,0,1:T(8,128)(2,1)}, u32[]{:S(2)}, u32[]{:S(2)}) collective-permute-start(bf16[2048,2,128]{2,0,1:T(8,128)(2,1)} %get-tuple-element.452), channel_id=1, source_target_pairs={{0,1},{1,2},{2,3},{3,4},{4,5},{5,6},{6,7},{7,0}} | collective-permute-start | bytes 3145736 | tf_op jit(solution)/shard_map/while/body/eval_jaxpr/ppermute | solution.py:60
  1503.7 71.2 %collective-permute-start = (bf16[2048,2,128]{2,0,1:T(8,128)(2,1)}, bf16[2048,2,128]{2,0,1:T(8,128)(2,1)S(1)}, u32[]{:S(2)}, u32[]{:S(2)}) collective-permute-start(bf16[2048,2,128]{2,0,1:T(8,128)(2,1)} %get-tuple-element.451), channel_id=1, source_target_pairs={{0,1},{1,2},{2,3},{3,4},{4,5},{5,6},{6,7},{7,0}} | collective-permute-start | bytes 3145736 | tf_op jit(solution)/shard_map/while/body/eval_jaxpr/ppermute | solution.py:59
  1765.3 17.3 copy-start
  1789.0 278.9 %collective-permute-start.2 = (f32[2,2048,128]{2,1,0:T(8,128)}, f32[2,2048,128]{2,1,0:T(8,128)}, u32[]{:S(2)}, u32[]{:S(2)}) collective-permute-start(f32[2,2048,128]{2,1,0:T(8,128)} %get-tuple-element.453), channel_id=1, source_target_pairs={{0,1},{1,2},{2,3},{3,4},{4,5},{5,6},{6,7},{7,0}} | collective-permute-start | bytes 6291464 | tf_op jit(solution)/shard_map/while/body/eval_jaxpr/ppermute | solution.py:61
  1789.0 282.1 %collective-permute-start.3 = (f32[2,2048,128]{2,1,0:T(8,128)}, f32[2,2048,128]{2,1,0:T(8,128)}, u32[]{:S(2)}, u32[]{:S(2)}) collective-permute-start(f32[2,2048,128]{2,1,0:T(8,128)} %get-tuple-element.454), channel_id=1, source_target_pairs={{0,1},{1,2},{2,3},{3,4},{4,5},{5,6},{6,7},{7,0}} | collective-permute-start | bytes 6291464 | tf_op jit(solution)/shard_map/while/body/eval_jaxpr/ppermute | solution.py:62
  1789.1 60.0 %collective-permute-start.1 = (bf16[2048,2,128]{2,0,1:T(8,128)(2,1)}, bf16[2048,2,128]{2,0,1:T(8,128)(2,1)}, u32[]{:S(2)}, u32[]{:S(2)}) collective-permute-start(bf16[2048,2,128]{2,0,1:T(8,128)(2,1)} %get-tuple-element.452), channel_id=1, source_target_pairs={{0,1},{1,2},{2,3},{3,4},{4,5},{5,6},{6,7},{7,0}} | collective-permute-start | bytes 3145736 | tf_op jit(solution)/shard_map/while/body/eval_jaxpr/ppermute | solution.py:60
  1789.1 71.2 %collective-permute-start = (bf16[2048,2,128]{2,0,1:T(8,128)(2,1)}, bf16[2048,2,128]{2,0,1:T(8,128)(2,1)S(1)}, u32[]{:S(2)}, u32[]{:S(2)}) collective-permute-start(bf16[2048,2,128]{2,0,1:T(8,128)(2,1)} %get-tuple-element.451), channel_id=1, source_target_pairs={{0,1},{1,2},{2,3},{3,4},{4,5},{5,6},{6,7},{7,0}} | collective-permute-start | bytes 3145736 | tf_op jit(solution)/shard_map/while/body/eval_jaxpr/ppermute | solution.py:59
  2050.7 17.3 copy-start
  2074.5 279.0 %collective-permute-start.2 = (f32[2,2048,128]{2,1,0:T(8,128)}, f32[2,2048,128]{2,1,0:T(8,128)}, u32[]{:S(2)}, u32[]{:S(2)}) collective-permute-start(f32[2,2048,128]{2,1,0:T(8,128)} %get-tuple-element.453), channel_id=1, source_target_pairs={{0,1},{1,2},{2,3},{3,4},{4,5},{5,6},{6,7},{7,0}} | collective-permute-start | bytes 6291464 | tf_op jit(solution)/shard_map/while/body/eval_jaxpr/ppermute | solution.py:61
  2074.5 282.1 %collective-permute-start.3 = (f32[2,2048,128]{2,1,0:T(8,128)}, f32[2,2048,128]{2,1,0:T(8,128)}, u32[]{:S(2)}, u32[]{:S(2)}) collective-permute-start(f32[2,2048,128]{2,1,0:T(8,128)} %get-tuple-element.454), channel_id=1, source_target_pairs={{0,1},{1,2},{2,3},{3,4},{4,5},{5,6},{6,7},{7,0}} | collective-permute-start | bytes 6291464 | tf_op jit(solution)/shard_map/while/body/eval_jaxpr/ppermute | solution.py:62
  2074.6 60.0 %collective-permute-start.1 = (bf16[2048,2,128]{2,0,1:T(8,128)(2,1)}, bf16[2048,2,128]{2,0,1:T(8,128)(2,1)}, u32[]{:S(2)}, u32[]{:S(2)}) collective-permute-start(bf16[2048,2,128]{2,0,1:T(8,128)(2,1)} %get-tuple-element.452), channel_id=1, source_target_pairs={{0,1},{1,2},{2,3},{3,4},{4,5},{5,6},{6,7},{7,0}} | collective-permute-start | bytes 3145736 | tf_op jit(solution)/shard_map/while/body/eval_jaxpr/ppermute | solution.py:60
  2074.6 71.2 %collective-permute-start = (bf16[2048,2,128]{2,0,1:T(8,128)(2,1)}, bf16[2048,2,128]{2,0,1:T(8,128)(2,1)S(1)}, u32[]{:S(2)}, u32[]{:S(2)}) collective-permute-start(bf16[2048,2,128]{2,0,1:T(8,128)(2,1)} %get-tuple-element.451), channel_id=1, source_target_pairs={{0,1},{1,2},{2,3},{3,4},{4,5},{5,6},{6,7},{7,0}} | collective-permute-start | bytes 3145736 | tf_op jit(solution)/shard_map/while/body/eval_jaxpr/ppermute | solution.py:59
  2336.2 17.3 copy-start
  2369.1 37.6 %collective-permute-start.4 = (f32[2,2048,128]{2,0,1:T(2,128)S(1)}, f32[2,2048,128]{2,0,1:T(2,128)S(1)}, u32[]{:S(2)}, u32[]{:S(2)}) collective-permute-start(f32[2,2048,128]{2,0,1:T(2,128)S(1)} %copy.33), channel_id=1, source_target_pairs={{0,1},{1,2},{2,3},{3,4},{4,5},{5,6},{6,7},{7,0}} | collective-permute-start | bytes 6291464 | tf_op jit(solution)/shard_map/ppermute | solution.py:68
  2373.6 33.1 %collective-permute-start.5 = (bf16[2,2048,128]{2,0,1:T(2,128)(2,1)S(1)}, bf16[2,2048,128]{2,0,1:T(2,128)(2,1)S(1)}, u32[]{:S(2)}, u32[]{:S(2)}) collective-permute-start(bf16[2,2048,128]{2,0,1:T(2,128)(2,1)S(1)} %copy.34), channel_id=1, source_target_pairs={{0,1},{1,2},{2,3},{3,4},{4,5},{5,6},{6,7},{7,0}} | collective-permute-start | bytes 3145736 | tf_op jit(solution)/shard_map/ppermute | solution.py:69
where the time goes:
time: 2420 us; the launch traced here: 2410 us
  matrix products  1550 us (64%)
  waiting for transfers between devices  518 us (21%)
  other arithmetic  166 us (7%)
  local copies, waits for them, and re-layouts  101 us (4%)
  loops' own time  63 us (3%)
    dot_general x8, matrix products, block_grads(): jnp.einsum('qkgd,skd->kqgs', do_blk, v_blk, preferred_element_type=jnp.fl...  466 us
    ppermute x7, waiting for transfers between devices, step_body(): v_cur = lax.ppermute(v_cur, ctx_axes, shift_perm)  415 us
    dot_general x8, matrix products, block_grads(): jnp.einsum('kqgs,qkgd->ksd', prob_b16, do_blk, preferred_element_type=jnp...  334 us
    dot_general x8, matrix products, block_grads(): jnp.einsum('qkgd,skd->kqgs', q_blk, k_blk, preferred_element_type=jnp.flo...  322 us
    dot_general x8, matrix products, block_grads(): jnp.einsum('kqgs,qkgd->ksd', dscore_b16, q_blk, preferred_element_type=jn...  233 us
    dot_general x8, matrix products, block_grads(): jnp.einsum('kqgs,skd->kqgd', dscore_b16, k_blk, preferred_element_type=jn...  199 us
    add x21, other arithmetic, step_body(): return (k_cur, v_cur, dk_cur + dk_part, dv_cur + dv_part, dq_cur + dq_part)  142 us
    ppermute x7, waiting for transfers between devices, step_body(): k_cur = lax.ppermute(k_cur, ctx_axes, shift_perm)  78.6 us
  transfers between devices with their start and end apart: 30, of which 15 were waited for; matrix products, arithmetic and copies ran while one was open for 59% of the time, Pallas kernels for 0%

commit v1 on v0

v1 whole, which is shorter than its diff:
```python
import functools
import math

import jax
import jax.numpy as jnp
from jax import lax
from jax.experimental import pallas as pl
from jax.experimental.pallas import tpu as pltpu
from jax.sharding import PartitionSpec as P

F32 = jnp.float32
BF16 = jnp.bfloat16
LANES = 128
SUB = 256


def split3(x):
    hi = lax.reduce_precision(x, 8, 7)
    mid = lax.reduce_precision(x - hi, 8, 7)
    return hi, mid, x - hi - mid


def dot_nn(a, b):
    return jnp.dot(a, b, preferred_element_type=F32)


def dot_nt(a, b):
    return lax.dot_general(a, b, (((1,), (1,)), ((), ())), preferred_element_type=F32)


def attn_kernel(cfg, *refs):
    local, half, scale, has_dq, has_dkv = cfg
    refs = list(refs)
    sel_ref = refs.pop(0)
    q_ref, qt_ref, do_ref, dot_ref, stat_ref, kv_ref, ones_ref = refs[:7]
    refs = refs[7:]
    dq_in = refs.pop(0) if has_dq else None
    dkv_in = refs.pop(0) if has_dkv else None
    dq_ref, dkv_ref, p_scr, ds_scr = refs
    d = q_ref.shape[-1]
    factor = scale * math.log2(math.e)

    @pl.when(pl.program_id(0) == 0)
    def _():
        dkv_ref[...] = dkv_in[...] if has_dkv else jnp.zeros_like(dkv_ref)

    dq_ref[...] = dq_in[...] if has_dq else jnp.zeros_like(dq_ref)

    def probs(qo, ko, width, row, keep):
        qs = pl.ds(qo + row, SUB)
        ks = pl.ds(ko, width)
        stat = stat_ref[0, qs, :]
        kt = jnp.concatenate([kv_ref[0:d, ks], ones_ref[0:LANES, 0:width]], axis=0)
        vt = jnp.concatenate([kv_ref[d : 2 * d, ks], ones_ref[LANES : 2 * LANES, 0:width]], axis=0)
        s = dot_nn(jnp.concatenate([q_ref[0, qs, :], stat], axis=1), kt)
        p = jnp.exp2(s * factor)
        if keep is not None:
            p = jnp.where(keep, p, 0.0)
        dp = dot_nn(jnp.concatenate([do_ref[0, qs, :], stat], axis=1), vt)
        rows = pl.ds(row, SUB)
        p_scr[rows, 0:width] = p.astype(BF16)
        ds_scr[rows, 0:width] = (p * dp).astype(BF16)

    def full_unit(qo, ko):
        for row in range(0, half, SUB):
            probs(qo, ko, half, row, None)
        qs = pl.ds(qo, half)
        ks = pl.ds(ko, half)
        p = p_scr[...]
        ds = ds_scr[...]
        dkv_ref[d : 2 * d, ks] += dot_nn(dot_ref[0, :, qs], p)
        dkv_ref[0:d, ks] += dot_nn(qt_ref[0, :, qs], ds)
        dq_ref[0, :, qs] += dot_nt(kv_ref[0:d, ks], ds)

    def diag_unit(off):
        for row in range(0, half, SUB):
            width = row + SUB
            shape = (SUB, width)
            keep = lax.broadcasted_iota(jnp.int32, shape, 0) + row >= lax.broadcasted_iota(jnp.int32, shape, 1)
            probs(off, off, width, row, keep)
        for col in range(0, half, SUB):
            qs = pl.ds(off + col, half - col)
            ks = pl.ds(off + col, SUB)
            p = p_scr[pl.ds(col, half - col), pl.ds(col, SUB)]
            ds = ds_scr[pl.ds(col, half - col), pl.ds(col, SUB)]
            dkv_ref[d : 2 * d, ks] += dot_nn(dot_ref[0, :, qs], p)
            dkv_ref[0:d, ks] += dot_nn(qt_ref[0, :, qs], ds)
        for row in range(0, half, SUB):
            ds = ds_scr[pl.ds(row, SUB), 0 : row + SUB]
            dq_ref[0, :, pl.ds(off + row, SUB)] += dot_nt(kv_ref[0:d, pl.ds(off, row + SUB)], ds)

    full_unit(half, 0)
    if local:
        diag_unit(0)
        diag_unit(half)
    else:
        off = pl.multiple_of(sel_ref[0] * half, half)
        full_unit(off, off)


def attn_step(sel, q, qt, do, dot, stat, kv, ones, dq, dkv, *, group, heads, local):
    d, tok = qt.shape[1], qt.shape[2]
    half = tok // 2
    first = group * heads
    row = pl.BlockSpec((1, tok, d), lambda h, s: (h + first, 0, 0))
    col = pl.BlockSpec((1, d, tok), lambda h, s: (h + first, 0, 0))
    own = pl.BlockSpec((1, d, tok), lambda h, s: (h, 0, 0))
    whole = lambda a: pl.BlockSpec(a.shape, lambda h, s: (0, 0))
    args = [sel, q, qt, do, dot, stat, kv, ones]
    in_specs = [row, col, row, col, row, whole(kv), whole(ones)]
    aliases = {}
    if dq is not None:
        aliases[len(args)] = 0
        args.append(dq)
        in_specs.append(own)
    if dkv is not None:
        aliases[len(args)] = 1
        args.append(dkv)
        in_specs.append(whole(dkv))
    cfg = (local, half, 1.0 / math.sqrt(d), dq is not None, dkv is not None)
    pairs = heads * half * half * 2
    return pl.pallas_call(
        functools.partial(attn_kernel, cfg),
        grid_spec=pltpu.PrefetchScalarGridSpec(
            num_scalar_prefetch=1,
            grid=(heads,),
            in_specs=in_specs,
            out_specs=[own, pl.BlockSpec((2 * d, tok), lambda h, s: (0, 0))],
            scratch_shapes=[pltpu.VMEM((half, half), BF16), pltpu.VMEM((half, half), BF16)],
        ),
        out_shape=[jax.ShapeDtypeStruct((heads, d, tok), F32), jax.ShapeDtypeStruct((2 * d, tok), F32)],
        input_output_aliases=aliases,
        compiler_params=pltpu.CompilerParams(vmem_limit_bytes=56 * 2**20),
        cost_estimate=pl.CostEstimate(flops=10 * pairs * d, bytes_accessed=heads * tok * d * 20, transcendentals=pairs),
        name="local_grads" if local else "step_grads",
    )(*args)


def solution(mesh):
    n_cx = mesh.shape["cx"]
    n_ctx = mesh.shape["cy"] * n_cx
    ctx_axes = ("cy", "cx")
    row_spec = P(("dp", "cy", "cx"), None, None)
    stat_spec = P(("dp", "cy", "cx"), None)
    ring = [r if r < n_cx else n_cx + (r - n_cx + n_cx // 2) % n_cx for r in range(n_ctx)] if n_cx == 4 else list(range(n_ctx))
    forward = [(ring[i], ring[(i + 1) % n_ctx]) for i in range(n_ctx)]
    backward = [(b, a) for a, b in forward]

    def local_grads(query_rows, key_rows, value_rows, out_rows, grad_out, log_sum_exp):
        tok, n_heads, d = query_rows.shape
        kv_heads = key_rows.shape[1]
        heads = n_heads // kv_heads
        half = tok // 2
        scale = 1.0 / math.sqrt(d)
        rank = lax.axis_index("cy") * n_cx + lax.axis_index("cx")
        ring_arr = jnp.array(ring, jnp.int32)
        pos = jnp.argmax(ring_arr == rank).astype(jnp.int32)

        q = query_rows.transpose(1, 0, 2)
        qt = query_rows.transpose(1, 2, 0)
        do = grad_out.transpose(1, 0, 2)
        dot = grad_out.transpose(1, 2, 0)
        delta = jnp.sum(grad_out.astype(F32) * out_rows.astype(F32), axis=-1)
        parts = [*split3(log_sum_exp / scale), *split3(delta)]
        lane = lax.broadcasted_iota(jnp.int32, (n_heads, tok, LANES), 2)
        stat = jnp.zeros((n_heads, tok, LANES), F32)
        for i, part in enumerate(parts):
            stat = jnp.where(lane == i, part.T[:, :, None], stat)
        stat = stat.astype(BF16)
        sub = lax.broadcasted_iota(jnp.int32, (2 * LANES, half), 0)
        minus = (sub < 3) | ((sub >= LANES + 3) & (sub < LANES + 6))
        ones = jnp.where(minus, -1.0, 0.0).astype(BF16)
        kt = key_rows.transpose(1, 2, 0)
        vt = value_rows.transpose(1, 2, 0)
        kv_own = [jnp.concatenate([kt[g], vt[g]], axis=0) for g in range(kv_heads)]

        perms = [forward if g % 2 == 0 else backward for g in range(kv_heads)]
        zero_sel = jnp.zeros((1,), jnp.int32)
        run = functools.partial(attn_step, q=q, qt=qt, do=do, dot=dot, stat=stat, ones=ones, heads=heads)
        dq = [None] * kv_heads
        own = [None] * kv_heads
        acc = [None] * kv_heads
        kv = list(kv_own)
        last = kv_heads - 1
        for g in range(last):
            dq[g], own[g] = run(zero_sel, kv=kv_own[g], dq=None, dkv=None, group=g, local=True)
        for t in range(1, n_ctx):
            for g in range(kv_heads):
                kv[g] = lax.ppermute(kv[g], ctx_axes, perms[g])
                shift = -t if g % 2 == 0 else t
                src = ring_arr[(pos + shift + n_ctx) % n_ctx]
                sel = (src > rank).astype(jnp.int32).reshape(1)
                if acc[g] is not None:
                    acc[g] = lax.ppermute(acc[g], ctx_axes, perms[g])
                dq[g], acc[g] = run(sel, kv=kv[g], dq=dq[g], dkv=acc[g], group=g, local=False)
        dq[last], own[last] = run(zero_sel, kv=kv_own[last], dq=dq[last], dkv=None, group=last, local=True)
        dks, dvs = [], []
        for g in range(kv_heads):
            total = lax.ppermute(acc[g], ctx_axes, perms[g]) + own[g]
            dks.append((total[:d] * scale).astype(BF16).T)
            dvs.append(total[d:].astype(BF16).T)
        grad_query = (jnp.concatenate(dq, axis=0) * scale).astype(BF16).transpose(2, 0, 1)
        return grad_query, jnp.stack(dks, axis=1), jnp.stack(dvs, axis=1)

    return jax.shard_map(local_grads, mesh=mesh, in_specs=(row_spec,) * 5 + (stat_spec,), out_specs=(row_spec,) * 3, check_vma=False)
```

time: 2420 us -> 703 us (0.29)
  matrix products: 1550 us -> 0 us
  Pallas kernels: 0 us -> 562 us
  waiting for transfers between devices: 518 us -> 0.07 us
  other arithmetic: 166 us -> 44.9 us
  loops' own time: 63 us -> 0 us
  local copies, waits for them, and re-layouts: 101 us -> 48.4 us
    dot_general x40 -> x0, matrix products: 1550 us -> none  [the longest x8 466 us: block_grads(): jnp.einsum('qkgd,skd->kqgs', do_blk, v_blk, preferred_element_type=jnp.fl...]
    pallas_call x0 -> x16, Pallas kernels: none -> 562 us  [attn_step(): pl.pallas_call(functools.partial(attn_kernel, cfg), grid_spec=pltpu.Prefe...]
    ppermute x30 -> x28, waiting for transfers between devices: 518 us -> 0.07 us  [the longest x14 0.04 us: local_grads(): kv[g] = lax.ppermute(kv[g], ctx_axes, perms[g])]
    add x22 -> x2, other arithmetic: 142 us -> 3.88 us  [local_grads(): total = lax.ppermute(acc[g], ctx_axes, perms[g]) + own[g]]
    another operation x8 -> x0, loops' own time: 63 us -> none  [the longest x7 55.9 us: step_body(): lax.cond(src_rank < ctx_rank, src_before, src_after, k_cur, v_cur)]
    concatenate x7 -> x0, local copies, waits for them, and re-layouts: 59.7 us -> none  [src_after(): return (jnp.concatenate([zero_pad, dq_part], axis=1), dk_part, dv_part)]
    unnamed x9 -> x47, local copies, waits for them, and re-layouts: 0.99 us -> 46.5 us
    while x32 -> x0, local copies, waits for them, and re-layouts: 33.9 us -> none
  transfers between devices with their start and end apart: 30 -> 28, of which waited for: 15 -> 0; matrix products, arithmetic and copies ran while one was open for 59% -> 10% of each run, Pallas kernels for 0% -> 81%
where the time goes in v1:
time: 703 us; the launch traced here: 694 us
  Pallas kernels  562 us (80%)
  local copies, waits for them, and re-layouts  48.4 us (7%)
  other arithmetic  44.9 us (6%)
  between operations  19.5 us (3%)
  starting transfers between devices  19.2 us (3%)
    pallas_call x16, Pallas kernels, attn_step(): pl.pallas_call(functools.partial(attn_kernel, cfg), grid_spec=pltpu.Prefe...  562 us
    unnamed x47, local copies, waits for them, and re-layouts  46.5 us
    convert_element_type x1, other arithmetic, local_grads(): stat = stat.astype(BF16)  22.5 us
  transfers between devices with their start and end apart: 28, of which 0 were waited for; matrix products, arithmetic and copies ran while one was open for 10% of the time, Pallas kernels for 81%

profile of v1, /device:TPU:0, one launch (start us, length us, event | category | flops | bytes accessed | tf_op | source)
XLA Modules:
  0.0 694.0 jit_solution(3063949975303270411)
XLA Ops:
  0.6 2.4 copy.38
  3.1 2.4 copy.39
  5.9 0.9 collective-permute-start
  6.9 2.0 collective-permute-start.13
  18.7 0.7 fusion.15
  20.1 8.7 %copy.37 = bf16[2048,12,128]{0,2,1:T(8,128)(2,1)} copy(bf16[2048,12,128]{2,0,1:T(8,128)(2,1)} %param.11) | data formatting | bytes 12582912 | tf_op args[4]
  28.8 8.0 %multiply_reduce_fusion = f32[2048,12]{0,1:T(8,128)S(1)} fusion(bf16[2048,12,128]{2,0,1:T(8,128)(2,1)} %param.10, bf16[2048,12,128]{2,0,1:T(8,128)(2,1)} %param.11), kind=kLoop, calls=%fused_computation.3 | loop fusion | flops 12558336 | bytes 12681216 | tf_op jit(solution)/shard_map/reduce_sum | solution.py:163
  36.8 8.6 %copy.36 = bf16[2048,12,128]{0,2,1:T(8,128)(2,1)} copy(bf16[2048,12,128]{2,0,1:T(8,128)(2,1)} %param.7) | data formatting | bytes 12582912 | tf_op args[0]
  46.0 22.5 %select_convert_fusion.refs_5_ = bf16[12,2048,128]{2,1,0:T(8,128)(2,1)} fusion(bf16[12,2048]{1,0:T(8,128)(2,1)S(1)} %get-tuple-element.81, bf16[12,2048]{1,0:T(8,128)(2,1)S(1)} %get-tuple-element.80, bf16[12,2048]{1,0:T(8,128)(2,1)S(1)} %get-tuple-element.79, bf16[12,2048]{1,0:T(8,128)(2,1)S(1)} %get-tuple-element.78, ...), kind=kLoop, calls=%fused_computation.2 | loop fusion | flops 18874368 | bytes 6587136 | tf_op jit(solution)/shard_map/convert_element_type | solution.py:169
  68.6 0.9 iota.110.refs_7_
  69.5 37.0 %local_grads.2 = (f32[6,128,2048]{2,1,0:T(8,128)}, f32[256,2048]{1,0:T(8,128)}) custom-call(s32[1]{0:T(128)} %constant.138.clone.1.refs_0_, bf16[12,2048,128]{2,1,0:T(8,128)(2,1)} %bitcast.93, bf16[12,128,2048]{2,1,0:T(8,128)(2,1)} %bitcast.125, bf16[12,2048,128]{2,1,0:T(8,128)(2,1)} %bitcast.77, bf16[12,128,2048]{2,1,0:T(8,128)(2,1)} %bitcast.109, ...), custom_call_target="tpu_custom_call" | custom-call | flops 16106127360 | bytes 31457280 | tf_op jit(solution)/shard_map/local_grads/pallas_call | solution.py:122
  106.5 34.3 %step_grads.14 = (f32[6,128,2048]{2,1,0:T(8,128)}, f32[256,2048]{1,0:T(8,128)}) custom-call(s32[1]{0:T(128)} %bitcast.25.refs_0_, bf16[12,2048,128]{2,1,0:T(8,128)(2,1)} %bitcast.94, bf16[12,128,2048]{2,1,0:T(8,128)(2,1)} %bitcast.126, bf16[12,2048,128]{2,1,0:T(8,128)(2,1)} %bitcast.78, ...), custom_call_target="tpu_custom_call", output_to_operand_aliasing={{0}: (8, {})} | custom-call | flops 16106127360 | bytes 31457280 | tf_op jit(solution)/shard_map/step_grads/pallas_call | solution.py:122
  140.8 0.8 collective-permute-start.7
  141.6 1.6 collective-permute-start.1
  143.1 33.8 %step_grads.21 = (f32[6,128,2048]{2,1,0:T(8,128)}, f32[256,2048]{1,0:T(8,128)}) custom-call(s32[1]{0:T(128)} %bitcast.41.refs_0_, bf16[12,2048,128]{2,1,0:T(8,128)(2,1)} %bitcast.95, bf16[12,128,2048]{2,1,0:T(8,128)(2,1)} %bitcast.127, bf16[12,2048,128]{2,1,0:T(8,128)(2,1)} %bitcast.79, bf16[12,128,2048]{2,1,0:T(8,128)(2,1)} %bitcast.111, ...), custom_call_target="tpu_custom_call" | custom-call | flops 16106127360 | bytes 31457280 | tf_op jit(solution)/shard_map/step_grads/pallas_call | solution.py:122
  178.9 35.0 %step_grads.15 = (f32[6,128,2048]{2,1,0:T(8,128)}, f32[256,2048]{1,0:T(8,128)}) custom-call(s32[1]{0:T(128)} %bitcast.23.refs_0_, bf16[12,2048,128]{2,1,0:T(8,128)(2,1)} %bitcast.96, bf16[12,128,2048]{2,1,0:T(8,128)(2,1)} %bitcast.128, bf16[12,2048,128]{2,1,0:T(8,128)(2,1)} %bitcast.80, ...), custom_call_target="tpu_custom_call", output_to_operand_aliasing={{0}: (8, {}), {1}: (9, {})} | custom-call | flops 16106127360 | bytes 31457280 | tf_op jit(solution)/shard_map/step_grads/pallas_call | solution.py:122
  213.9 1.6 collective-permute-start.8
  215.5 1.0 copy-done.14
  217.1 34.9 %step_grads.22 = (f32[6,128,2048]{2,1,0:T(8,128)}, f32[256,2048]{1,0:T(8,128)}) custom-call(s32[1]{0:T(128)} %bitcast.39.refs_0_, bf16[12,2048,128]{2,1,0:T(8,128)(2,1)} %bitcast.97, bf16[12,128,2048]{2,1,0:T(8,128)(2,1)} %bitcast.129, bf16[12,2048,128]{2,1,0:T(8,128)(2,1)} %bitcast.81, ...), custom_call_target="tpu_custom_call", output_to_operand_aliasing={{0}: (8, {}), {1}: (9, {})} | custom-call | flops 16106127360 | bytes 31457280 | tf_op jit(solution)/shard_map/step_grads/pallas_call | solution.py:122
  254.5 35.0 %step_grads.16 = (f32[6,128,2048]{2,1,0:T(8,128)}, f32[256,2048]{1,0:T(8,128)}) custom-call(s32[1]{0:T(128)} %bitcast.21.refs_0_, bf16[12,2048,128]{2,1,0:T(8,128)(2,1)} %bitcast.98, bf16[12,128,2048]{2,1,0:T(8,128)(2,1)} %bitcast.130, bf16[12,2048,128]{2,1,0:T(8,128)(2,1)} %bitcast.82, ...), custom_call_target="tpu_custom_call", output_to_operand_aliasing={{0}: (8, {}), {1}: (9, {})} | custom-call | flops 16106127360 | bytes 31457280 | tf_op jit(solution)/shard_map/step_grads/pallas_call | solution.py:122
  289.5 1.1 collective-permute-start.9
  290.6 1.0 copy-done.15
  292.2 34.9 %step_grads.23 = (f32[6,128,2048]{2,1,0:T(8,128)}, f32[256,2048]{1,0:T(8,128)}) custom-call(s32[1]{0:T(128)} %bitcast.37.refs_0_, bf16[12,2048,128]{2,1,0:T(8,128)(2,1)} %bitcast.99, bf16[12,128,2048]{2,1,0:T(8,128)(2,1)} %bitcast.131, bf16[12,2048,128]{2,1,0:T(8,128)(2,1)} %bitcast.83, ...), custom_call_target="tpu_custom_call", output_to_operand_aliasing={{0}: (8, {}), {1}: (9, {})} | custom-call | flops 16106127360 | bytes 31457280 | tf_op jit(solution)/shard_map/step_grads/pallas_call | solution.py:122
  329.6 35.2 %step_grads.17 = (f32[6,128,2048]{2,1,0:T(8,128)}, f32[256,2048]{1,0:T(8,128)}) custom-call(s32[1]{0:T(128)} %bitcast.19.refs_0_, bf16[12,2048,128]{2,1,0:T(8,128)(2,1)} %bitcast.100, bf16[12,128,2048]{2,1,0:T(8,128)(2,1)} %bitcast.132, bf16[12,2048,128]{2,1,0:T(8,128)(2,1)} %bitcast.84, ...), custom_call_target="tpu_custom_call", output_to_operand_aliasing={{0}: (8, {}), {1}: (9, {})} | custom-call | flops 16106127360 | bytes 31457280 | tf_op jit(solution)/shard_map/step_grads/pallas_call | solution.py:122
  364.9 1.5 collective-permute-start.10
  366.4 1.0 copy-done.16
  368.1 34.9 %step_grads.24 = (f32[6,128,2048]{2,1,0:T(8,128)}, f32[256,2048]{1,0:T(8,128)}) custom-call(s32[1]{0:T(128)} %bitcast.35.refs_0_, bf16[12,2048,128]{2,1,0:T(8,128)(2,1)} %bitcast.101, bf16[12,128,2048]{2,1,0:T(8,128)(2,1)} %bitcast.133, bf16[12,2048,128]{2,1,0:T(8,128)(2,1)} %bitcast.85, ...), custom_call_target="tpu_custom_call", output_to_operand_aliasing={{0}: (8, {}), {1}: (9, {})} | custom-call | flops 16106127360 | bytes 31457280 | tf_op jit(solution)/shard_map/step_grads/pallas_call | solution.py:122
  405.1 35.0 %step_grads.18 = (f32[6,128,2048]{2,1,0:T(8,128)}, f32[256,2048]{1,0:T(8,128)}) custom-call(s32[1]{0:T(128)} %bitcast.17.refs_0_, bf16[12,2048,128]{2,1,0:T(8,128)(2,1)} %bitcast.102, bf16[12,128,2048]{2,1,0:T(8,128)(2,1)} %bitcast.134, bf16[12,2048,128]{2,1,0:T(8,128)(2,1)} %bitcast.86, ...), custom_call_target="tpu_custom_call", output_to_operand_aliasing={{0}: (8, {}), {1}: (9, {})} | custom-call | flops 16106127360 | bytes 31457280 | tf_op jit(solution)/shard_map/step_grads/pallas_call | solution.py:122
  440.1 1.5 collective-permute-start.11
  441.6 1.0 copy-done.17
  443.3 34.9 %step_grads.25 = (f32[6,128,2048]{2,1,0:T(8,128)}, f32[256,2048]{1,0:T(8,128)}) custom-call(s32[1]{0:T(128)} %bitcast.33.refs_0_, bf16[12,2048,128]{2,1,0:T(8,128)(2,1)} %bitcast.103, bf16[12,128,2048]{2,1,0:T(8,128)(2,1)} %bitcast.135, bf16[12,2048,128]{2,1,0:T(8,128)(2,1)} %bitcast.87, ...), custom_call_target="tpu_custom_call", output_to_operand_aliasing={{0}: (8, {}), {1}: (9, {})} | custom-call | flops 16106127360 | bytes 31457280 | tf_op jit(solution)/shard_map/step_grads/pallas_call | solution.py:122
  480.2 1.0 copy-done.12
  481.1 34.9 %step_grads.19 = (f32[6,128,2048]{2,1,0:T(8,128)}, f32[256,2048]{1,0:T(8,128)}) custom-call(s32[1]{0:T(128)} %bitcast.15.refs_0_, bf16[12,2048,128]{2,1,0:T(8,128)(2,1)} %bitcast.104, bf16[12,128,2048]{2,1,0:T(8,128)(2,1)} %bitcast.136, bf16[12,2048,128]{2,1,0:T(8,128)(2,1)} %bitcast.88, ...), custom_call_target="tpu_custom_call", output_to_operand_aliasing={{0}: (8, {}), {1}: (9, {})} | custom-call | flops 16106127360 | bytes 31457280 | tf_op jit(solution)/shard_map/step_grads/pallas_call | solution.py:122
  516.6 1.0 copy-done.18
  518.3 34.8 %step_grads.26 = (f32[6,128,2048]{2,1,0:T(8,128)}, f32[256,2048]{1,0:T(8,128)}) custom-call(s32[1]{0:T(128)} %bitcast.31.refs_0_, bf16[12,2048,128]{2,1,0:T(8,128)(2,1)} %bitcast.105, bf16[12,128,2048]{2,1,0:T(8,128)(2,1)} %bitcast.137, bf16[12,2048,128]{2,1,0:T(8,128)(2,1)} %bitcast.89, ...), custom_call_target="tpu_custom_call", output_to_operand_aliasing={{0}: (8, {}), {1}: (9, {})} | custom-call | flops 16106127360 | bytes 31457280 | tf_op jit(solution)/shard_map/step_grads/pallas_call | solution.py:122
  553.1 1.2 collective-permute-start.25
  556.2 35.0 %step_grads.20 = (f32[6,128,2048]{2,1,0:T(8,128)}, f32[256,2048]{1,0:T(8,128)}) custom-call(s32[1]{0:T(128)} %bitcast.1.refs_0_, bf16[12,2048,128]{2,1,0:T(8,128)(2,1)} %bitcast.106, bf16[12,128,2048]{2,1,0:T(8,128)(2,1)} %bitcast.138, bf16[12,2048,128]{2,1,0:T(8,128)(2,1)} %bitcast.90, ...), custom_call_target="tpu_custom_call", output_to_operand_aliasing={{0}: (8, {}), {1}: (9, {})} | custom-call | flops 16106127360 | bytes 31457280 | tf_op jit(solution)/shard_map/step_grads/pallas_call | solution.py:122
  591.3 0.9 copy-done.19
  592.2 0.7 copy-done.11
  592.9 34.9 %step_grads.27 = (f32[6,128,2048]{2,1,0:T(8,128)}, f32[256,2048]{1,0:T(8,128)}) custom-call(s32[1]{0:T(128)} %bitcast.29.refs_0_, bf16[12,2048,128]{2,1,0:T(8,128)(2,1)} %bitcast.107, bf16[12,128,2048]{2,1,0:T(8,128)(2,1)} %bitcast.139, bf16[12,2048,128]{2,1,0:T(8,128)(2,1)} %bitcast.91, ...), custom_call_target="tpu_custom_call", output_to_operand_aliasing={{0}: (8, {}), {1}: (9, {})} | custom-call | flops 16106127360 | bytes 31457280 | tf_op jit(solution)/shard_map/step_grads/pallas_call | solution.py:122
  627.8 1.7 collective-permute-start.27
  629.6 37.5 %local_grads.3 = (f32[6,128,2048]{2,1,0:T(8,128)}, f32[256,2048]{1,0:T(8,128)}) custom-call(s32[1]{0:T(128)} %constant.138.clone.1.refs_0_, bf16[12,2048,128]{2,1,0:T(8,128)(2,1)} %bitcast.108, bf16[12,128,2048]{2,1,0:T(8,128)(2,1)} %bitcast.140, bf16[12,2048,128]{2,1,0:T(8,128)(2,1)} %bitcast.92, ...), custom_call_target="tpu_custom_call", output_to_operand_aliasing={{0}: (8, {})} | custom-call | flops 16106127360 | bytes 31457280 | tf_op jit(solution)/shard_map/local_grads/pallas_call | solution.py:122
  667.1 9.1 %fusion.1 = bf16[2048,12,128]{0,2,1:T(8,128)(2,1)} fusion(f32[6,128,2048]{2,1,0:T(8,128)} %get-tuple-element.64, f32[6,128,2048]{2,1,0:T(8,128)} %get-tuple-element.50), kind=kLoop, calls=%fused_computation.4 | loop fusion | flops 9437184 | bytes 18874368 | tf_op jit(solution)/shard_map/transpose | solution.py:202
  676.2 8.8 %copy.40 = bf16[2048,12,128]{2,0,1:T(8,128)(2,1)} copy(bf16[2048,12,128]{0,2,1:T(8,128)(2,1)} %fusion.1) | data formatting | bytes 12582912
  685.0 2.0 add.221
  687.2 1.9 add.222
  689.4 2.0 copy.42
  691.5 2.0 copy.41
  (94 shorter events, 11.2 us)
Async XLA Ops:
  0.6 8.3 %copy-start.5 = (s32[8]{0:T(128)S(1)}, s32[8]{0:T(128)}, u32[]{:S(2)}) copy-start(s32[8]{0:T(128)} %constant.147.clone) | copy-start | bytes 100
  5.9 22.9 %copy-start.3 = (bf16[256,2048]{1,0:T(8,128)(2,1)}, bf16[256,2048]{1,0:T(8,128)(2,1)S(1)}, u32[]{:S(2)}) copy-start(bf16[256,2048]{1,0:T(8,128)(2,1)S(1)} %pad_maximum_fusion.refs_6_) | copy-start | bytes 3145732
  5.9 100.5 %collective-permute-start = (bf16[256,2048]{1,0:T(8,128)(2,1)S(1)}, bf16[256,2048]{1,0:T(8,128)(2,1)}, u32[]{:S(2)}, u32[]{:S(2)}) collective-permute-start(bf16[256,2048]{1,0:T(8,128)(2,1)S(1)} %pad_maximum_fusion.refs_6_), channel_id=1, source_target_pairs={{0,1},{1,2},{2,3},{3,6},{6,7},{7,4},{4,5},{5,0}} | collective-permute-start | bytes 3145736 | tf_op jit(solution)/shard_map/ppermute | solution.py:189
  6.9 21.9 %copy-start.2 = (bf16[256,2048]{1,0:T(8,128)(2,1)}, bf16[256,2048]{1,0:T(8,128)(2,1)S(1)}, u32[]{:S(2)}) copy-start(bf16[256,2048]{1,0:T(8,128)(2,1)S(1)} %pad_maximum_fusion.1.refs_6_) | copy-start | bytes 3145732
  6.9 136.2 %collective-permute-start.13 = (bf16[256,2048]{1,0:T(8,128)(2,1)S(1)}, bf16[256,2048]{1,0:T(8,128)(2,1)}, u32[]{:S(2)}, u32[]{:S(2)}) collective-permute-start(bf16[256,2048]{1,0:T(8,128)(2,1)S(1)} %pad_maximum_fusion.1.refs_6_), channel_id=1, source_target_pairs={{1,0},{2,1},{3,2},{6,3},{7,6},{4,7},{5,4},{0,5}} | collective-permute-start | bytes 3145736 | tf_op jit(solution)/shard_map/ppermute | solution.py:189
  28.8 8.0 %copy-start.4 = (f32[2048,12]{0,1:T(8,128)S(1)}, f32[2048,12]{0,1:T(8,128)}, u32[]{:S(2)}) copy-start(f32[2048,12]{0,1:T(8,128)} %param.12) | copy-start | bytes 294916
  140.8 38.1 %collective-permute-start.7 = (f32[256,2048]{1,0:T(8,128)}, f32[256,2048]{1,0:T(8,128)}, u32[]{:S(2)}, u32[]{:S(2)}) collective-permute-start(f32[256,2048]{1,0:T(8,128)} %get-tuple-element.39), channel_id=1, source_target_pairs={{0,1},{1,2},{2,3},{3,6},{6,7},{7,4},{4,5},{5,0}} | collective-permute-start | bytes 6291464 | tf_op jit(solution)/shard_map/ppermute | solution.py:194
  141.6 36.8 %collective-permute-start.1 = (bf16[256,2048]{1,0:T(8,128)(2,1)}, bf16[256,2048]{1,0:T(8,128)(2,1)}, u32[]{:S(2)}, u32[]{:S(2)}) collective-permute-start(bf16[256,2048]{1,0:T(8,128)(2,1)} %collective-permute-done.refs_6_), channel_id=1, source_target_pairs={{0,1},{1,2},{2,3},{3,6},{6,7},{7,4},{4,5},{5,0}} | collective-permute-start | bytes 3145736 | tf_op jit(solution)/shard_map/ppermute | solution.py:189
  176.9 38.6 %collective-permute-start.20 = (f32[256,2048]{1,0:T(8,128)}, f32[256,2048]{1,0:T(8,128)S(1)}, u32[]{:S(2)}, u32[]{:S(2)}) collective-permute-start(f32[256,2048]{1,0:T(8,128)} %get-tuple-element.52), channel_id=1, source_target_pairs={{1,0},{2,1},{3,2},{6,3},{7,6},{4,7},{5,4},{0,5}} | collective-permute-start | bytes 6291464 | tf_op jit(solution)/shard_map/ppermute | solution.py:194
  178.4 37.1 %collective-permute-start.14 = (bf16[256,2048]{1,0:T(8,128)(2,1)}, bf16[256,2048]{1,0:T(8,128)(2,1)S(1)}, u32[]{:S(2)}, u32[]{:S(2)}) collective-permute-start(bf16[256,2048]{1,0:T(8,128)(2,1)} %collective-permute-done.13.refs_6_), channel_id=1, source_target_pairs={{1,0},{2,1},{3,2},{6,3},{7,6},{4,7},{5,4},{0,5}} | collective-permute-start | bytes 3145736 | tf_op jit(solution)/shard_map/ppermute | solution.py:189
  178.4 75.1 %collective-permute-start.2 = (bf16[256,2048]{1,0:T(8,128)(2,1)}, bf16[256,2048]{1,0:T(8,128)(2,1)S(1)}, u32[]{:S(2)}, u32[]{:S(2)}) collective-permute-start(bf16[256,2048]{1,0:T(8,128)(2,1)} %collective-permute-done.1.refs_6_), channel_id=1, source_target_pairs={{0,1},{1,2},{2,3},{3,6},{6,7},{7,4},{4,5},{5,0}} | collective-permute-start | bytes 3145736 | tf_op jit(solution)/shard_map/ppermute | solution.py:189
  213.9 40.1 %collective-permute-start.8 = (f32[256,2048]{1,0:T(8,128)}, f32[256,2048]{1,0:T(8,128)}, u32[]{:S(2)}, u32[]{:S(2)}) collective-permute-start(f32[256,2048]{1,0:T(8,128)} %get-tuple-element.41), channel_id=1, source_target_pairs={{0,1},{1,2},{2,3},{3,6},{6,7},{7,4},{4,5},{5,0}} | collective-permute-start | bytes 6291464 | tf_op jit(solution)/shard_map/ppermute | solution.py:194
  215.5 1.0 copy-start.14
  215.5 1.7 copy-start.6
  252.0 38.6 %collective-permute-start.21 = (f32[256,2048]{1,0:T(8,128)}, f32[256,2048]{1,0:T(8,128)S(1)}, u32[]{:S(2)}, u32[]{:S(2)}) collective-permute-start(f32[256,2048]{1,0:T(8,128)} %get-tuple-element.54), channel_id=1, source_target_pairs={{1,0},{2,1},{3,2},{6,3},{7,6},{4,7},{5,4},{0,5}} | collective-permute-start | bytes 6291464 | tf_op jit(solution)/shard_map/ppermute | solution.py:194
  253.5 37.1 %collective-permute-start.15 = (bf16[256,2048]{1,0:T(8,128)(2,1)}, bf16[256,2048]{1,0:T(8,128)(2,1)S(1)}, u32[]{:S(2)}, u32[]{:S(2)}) collective-permute-start(bf16[256,2048]{1,0:T(8,128)(2,1)} %copy-done.14), channel_id=1, source_target_pairs={{1,0},{2,1},{3,2},{6,3},{7,6},{4,7},{5,4},{0,5}} | collective-permute-start | bytes 3145736 | tf_op jit(solution)/shard_map/ppermute | solution.py:189
  253.5 1.0 copy-start.13
  253.5 76.0 %collective-permute-start.3 = (bf16[256,2048]{1,0:T(8,128)(2,1)S(1)}, bf16[256,2048]{1,0:T(8,128)(2,1)}, u32[]{:S(2)}, u32[]{:S(2)}) collective-permute-start(bf16[256,2048]{1,0:T(8,128)(2,1)S(1)} %collective-permute-done.2.refs_6_), channel_id=1, source_target_pairs={{0,1},{1,2},{2,3},{3,6},{6,7},{7,4},{4,5},{5,0}} | collective-permute-start | bytes 3145736 | tf_op jit(solution)/shard_map/ppermute | solution.py:189
  289.5 40.2 %collective-permute-start.9 = (f32[256,2048]{1,0:T(8,128)}, f32[256,2048]{1,0:T(8,128)}, u32[]{:S(2)}, u32[]{:S(2)}) collective-permute-start(f32[256,2048]{1,0:T(8,128)} %get-tuple-element.43), channel_id=1, source_target_pairs={{0,1},{1,2},{2,3},{3,6},{6,7},{7,4},{4,5},{5,0}} | collective-permute-start | bytes 6291464 | tf_op jit(solution)/shard_map/ppermute | solution.py:194
  290.6 1.0 copy-start.15
  290.6 1.7 copy-start.7
  327.1 39.3 %collective-permute-start.22 = (f32[256,2048]{1,0:T(8,128)}, f32[256,2048]{1,0:T(8,128)S(1)}, u32[]{:S(2)}, u32[]{:S(2)}) collective-permute-start(f32[256,2048]{1,0:T(8,128)} %get-tuple-element.56), channel_id=1, source_target_pairs={{1,0},{2,1},{3,2},{6,3},{7,6},{4,7},{5,4},{0,5}} | collective-permute-start | bytes 6291464 | tf_op jit(solution)/shard_map/ppermute | solution.py:194
  329.1 37.3 %collective-permute-start.16 = (bf16[256,2048]{1,0:T(8,128)(2,1)}, bf16[256,2048]{1,0:T(8,128)(2,1)S(1)}, u32[]{:S(2)}, u32[]{:S(2)}) collective-permute-start(bf16[256,2048]{1,0:T(8,128)(2,1)} %copy-done.15), channel_id=1, source_target_pairs={{1,0},{2,1},{3,2},{6,3},{7,6},{4,7},{5,4},{0,5}} | collective-permute-start | bytes 3145736 | tf_op jit(solution)/shard_map/ppermute | solution.py:189
  329.6 75.5 %collective-permute-start.4 = (bf16[256,2048]{1,0:T(8,128)(2,1)}, bf16[256,2048]{1,0:T(8,128)(2,1)}, u32[]{:S(2)}, u32[]{:S(2)}) collective-permute-start(bf16[256,2048]{1,0:T(8,128)(2,1)} %collective-permute-done.3.refs_6_), channel_id=1, source_target_pairs={{0,1},{1,2},{2,3},{3,6},{6,7},{7,4},{4,5},{5,0}} | collective-permute-start | bytes 3145736 | tf_op jit(solution)/shard_map/ppermute | solution.py:189
  364.9 40.2 %collective-permute-start.10 = (f32[256,2048]{1,0:T(8,128)}, f32[256,2048]{1,0:T(8,128)}, u32[]{:S(2)}, u32[]{:S(2)}) collective-permute-start(f32[256,2048]{1,0:T(8,128)} %get-tuple-element.45), channel_id=1, source_target_pairs={{0,1},{1,2},{2,3},{3,6},{6,7},{7,4},{4,5},{5,0}} | collective-permute-start | bytes 6291464 | tf_op jit(solution)/shard_map/ppermute | solution.py:194
  366.4 1.0 copy-start.16
  366.4 1.7 copy-start.8
  402.9 38.6 %collective-permute-start.23 = (f32[256,2048]{1,0:T(8,128)}, f32[256,2048]{1,0:T(8,128)S(1)}, u32[]{:S(2)}, u32[]{:S(2)}) collective-permute-start(f32[256,2048]{1,0:T(8,128)} %get-tuple-element.58), channel_id=1, source_target_pairs={{1,0},{2,1},{3,2},{6,3},{7,6},{4,7},{5,4},{0,5}} | collective-permute-start | bytes 6291464 | tf_op jit(solution)/shard_map/ppermute | solution.py:194
  404.6 37.0 %collective-permute-start.17 = (bf16[256,2048]{1,0:T(8,128)(2,1)}, bf16[256,2048]{1,0:T(8,128)(2,1)S(1)}, u32[]{:S(2)}, u32[]{:S(2)}) collective-permute-start(bf16[256,2048]{1,0:T(8,128)(2,1)} %copy-done.16), channel_id=1, source_target_pairs={{1,0},{2,1},{3,2},{6,3},{7,6},{4,7},{5,4},{0,5}} | collective-permute-start | bytes 3145736 | tf_op jit(solution)/shard_map/ppermute | solution.py:189
  405.1 75.1 %collective-permute-start.5 = (bf16[256,2048]{1,0:T(8,128)(2,1)}, bf16[256,2048]{1,0:T(8,128)(2,1)S(1)}, u32[]{:S(2)}, u32[]{:S(2)}) collective-permute-start(bf16[256,2048]{1,0:T(8,128)(2,1)} %collective-permute-done.4.refs_6_), channel_id=1, source_target_pairs={{0,1},{1,2},{2,3},{3,6},{6,7},{7,4},{4,5},{5,0}} | collective-permute-start | bytes 3145736 | tf_op jit(solution)/shard_map/ppermute | solution.py:189
  440.1 40.1 %collective-permute-start.11 = (f32[256,2048]{1,0:T(8,128)}, f32[256,2048]{1,0:T(8,128)}, u32[]{:S(2)}, u32[]{:S(2)}) collective-permute-start(f32[256,2048]{1,0:T(8,128)} %get-tuple-element.47), channel_id=1, source_target_pairs={{0,1},{1,2},{2,3},{3,6},{6,7},{7,4},{4,5},{5,0}} | collective-permute-start | bytes 6291464 | tf_op jit(solution)/shard_map/ppermute | solution.py:194
  441.6 1.0 copy-start.17
  441.6 1.7 copy-start.9
  478.1 38.5 %collective-permute-start.24 = (f32[256,2048]{1,0:T(8,128)}, f32[256,2048]{1,0:T(8,128)S(1)}, u32[]{:S(2)}, u32[]{:S(2)}) collective-permute-start(f32[256,2048]{1,0:T(8,128)} %get-tuple-element.60), channel_id=1, source_target_pairs={{1,0},{2,1},{3,2},{6,3},{7,6},{4,7},{5,4},{0,5}} | collective-permute-start | bytes 6291464 | tf_op jit(solution)/shard_map/ppermute | solution.py:194
  479.6 37.0 %collective-permute-start.18 = (bf16[256,2048]{1,0:T(8,128)(2,1)}, bf16[256,2048]{1,0:T(8,128)(2,1)S(1)}, u32[]{:S(2)}, u32[]{:S(2)}) collective-permute-start(bf16[256,2048]{1,0:T(8,128)(2,1)} %copy-done.17), channel_id=1, source_target_pairs={{1,0},{2,1},{3,2},{6,3},{7,6},{4,7},{5,4},{0,5}} | collective-permute-start | bytes 3145736 | tf_op jit(solution)/shard_map/ppermute | solution.py:189
  480.1 1.0 copy-start.12
  480.1 76.0 %collective-permute-start.6 = (bf16[256,2048]{1,0:T(8,128)(2,1)S(1)}, bf16[256,2048]{1,0:T(8,128)(2,1)}, u32[]{:S(2)}, u32[]{:S(2)}) collective-permute-start(bf16[256,2048]{1,0:T(8,128)(2,1)S(1)} %collective-permute-done.5.refs_6_), channel_id=1, source_target_pairs={{0,1},{1,2},{2,3},{3,6},{6,7},{7,4},{4,5},{5,0}} | collective-permute-start | bytes 3145736 | tf_op jit(solution)/shard_map/ppermute | solution.py:189
  516.1 40.1 %collective-permute-start.12 = (f32[256,2048]{1,0:T(8,128)}, f32[256,2048]{1,0:T(8,128)}, u32[]{:S(2)}, u32[]{:S(2)}) collective-permute-start(f32[256,2048]{1,0:T(8,128)} %get-tuple-element.49), channel_id=1, source_target_pairs={{0,1},{1,2},{2,3},{3,6},{6,7},{7,4},{4,5},{5,0}} | collective-permute-start | bytes 6291464 | tf_op jit(solution)/shard_map/ppermute | solution.py:194
  516.6 1.0 copy-start.18
  516.6 1.6 copy-start.10
  553.1 38.1 %collective-permute-start.25 = (f32[256,2048]{1,0:T(8,128)}, f32[256,2048]{1,0:T(8,128)S(1)}, u32[]{:S(2)}, u32[]{:S(2)}) collective-permute-start(f32[256,2048]{1,0:T(8,128)} %get-tuple-element.62), channel_id=1, source_target_pairs={{1,0},{2,1},{3,2},{6,3},{7,6},{4,7},{5,4},{0,5}} | collective-permute-start | bytes 6291464 | tf_op jit(solution)/shard_map/ppermute | solution.py:194
  555.7 35.6 %collective-permute-start.19 = (bf16[256,2048]{1,0:T(8,128)(2,1)}, bf16[256,2048]{1,0:T(8,128)(2,1)S(1)}, u32[]{:S(2)}, u32[]{:S(2)}) collective-permute-start(bf16[256,2048]{1,0:T(8,128)(2,1)} %copy-done.18), channel_id=1, source_target_pairs={{1,0},{2,1},{3,2},{6,3},{7,6},{4,7},{5,4},{0,5}} | collective-permute-start | bytes 3145736 | tf_op jit(solution)/shard_map/ppermute | solution.py:189
  591.2 93.8 %collective-permute-start.26 = (f32[256,2048]{1,0:T(8,128)}, f32[256,2048]{1,0:T(8,128)}, u32[]{:S(2)}, u32[]{:S(2)}) collective-permute-start(f32[256,2048]{1,0:T(8,128)} %get-tuple-element.65), channel_id=1, source_target_pairs={{0,1},{1,2},{2,3},{3,6},{6,7},{7,4},{4,5},{5,0}} | collective-permute-start | bytes 6291464 | tf_op jit(solution)/shard_map/ppermute | solution.py:199
  591.2 1.0 copy-start.19
  591.2 1.7 copy-start.11
  627.8 59.3 %collective-permute-start.27 = (f32[256,2048]{1,0:T(8,128)}, f32[256,2048]{1,0:T(8,128)}, u32[]{:S(2)}, u32[]{:S(2)}) collective-permute-start(f32[256,2048]{1,0:T(8,128)} %get-tuple-element.67), channel_id=1, source_target_pairs={{1,0},{2,1},{3,2},{6,3},{7,6},{4,7},{5,4},{0,5}} | collective-permute-start | bytes 6291464 | tf_op jit(solution)/shard_map/ppermute | solution.py:199
  676.2 8.8 %copy-start = (f32[256,2048]{1,0:T(8,128)S(1)}, f32[256,2048]{1,0:T(8,128)}, u32[]{:S(2)}) copy-start(f32[256,2048]{1,0:T(8,128)} %get-tuple-element.66) | copy-start | bytes 6291460
  685.0 2.2 copy-start.1

commit v2 on v0

v2 whole, which is shorter than its diff:
```python
import functools
import math

import jax
import jax.numpy as jnp
from jax import lax
from jax.experimental import pallas as pl
from jax.experimental.pallas import tpu as pltpu
from jax.sharding import PartitionSpec as P

F32 = jnp.float32
BF16 = jnp.bfloat16
LANES = 128
SUB = 256
PARTS = 3
MESH = pl.DeviceIdType.MESH


def split3(x):
    hi = lax.reduce_precision(x, 8, 7)
    mid = lax.reduce_precision(x - hi, 8, 7)
    return hi, mid, x - hi - mid


def dot_nn(a, b):
    return jnp.dot(a, b, preferred_element_type=F32)


def dot_nt(a, b):
    return lax.dot_general(a, b, (((1,), (1,)), ((), ())), preferred_element_type=F32)


def ring_kernel(dims, q_hbm, do_hbm, stat_hbm, kv_own, dq_hbm, own_hbm, kv_hbm, dkv_hbm,
                q_v, do_v, qt_v, dot_v, stat_v, dq_v, kv_v, acc, tmp, p_scr, ds_scr,
                in_sem, stat_sem, out_sem, load_sem, tmp_sem, own_sem, kv_send, kv_recv, dkv_send, dkv_recv):
    n_cy, n_cx, groups, heads, tok, d = dims
    n = n_cy * n_cx
    half = tok // 2
    scale = 1.0 / math.sqrt(d)
    factor = scale * math.log2(math.e)
    dp = lax.axis_index("dp")
    rank = lax.axis_index("cy") * n_cx + lax.axis_index("cx")

    def ring(i):
        return i // n_cx * n_cx + (i % n_cx + n_cx // 2 * (i // n_cx)) % n_cx

    pos = ring(rank)
    targets = []
    for step in (1, n - 1):
        other = ring((pos + step) % n)
        targets.append((dp, other // n_cx, other % n_cx))

    def source_later(t, g):
        src = ring((pos + (n - t if g == 0 else t)) % n)
        return (src - rank + n - 1) // n

    barrier = pltpu.get_barrier_semaphore()
    for target in targets:
        pl.semaphore_signal(barrier, inc=1, device_id=target, device_id_type=MESH)
    pl.semaphore_wait(barrier, 2)

    def send_kv(g, t):
        src = kv_own.at[g] if isinstance(t, int) and t == 0 else kv_hbm.at[g, t - 1]
        return pltpu.make_async_remote_copy(src_ref=src, dst_ref=kv_hbm.at[g, t], send_sem=kv_send.at[g, t],
                                            recv_sem=kv_recv.at[g, t], device_id=targets[g], device_id_type=MESH)

    def wait_kv(g, t):
        slot = kv_hbm.at[g, t]
        pltpu.make_async_remote_copy(src_ref=slot, dst_ref=slot, send_sem=kv_send.at[g, t], recv_sem=kv_recv.at[g, t],
                                     device_id=targets[g], device_id_type=MESH).wait_recv()

    def send_dkv(g, t):
        return pltpu.make_async_remote_copy(src_ref=acc.at[g], dst_ref=dkv_hbm.at[g, t - 1], send_sem=dkv_send.at[g, t - 1],
                                            recv_sem=dkv_recv.at[g, t - 1], device_id=targets[g], device_id_type=MESH)

    def load_kv(g, t):
        return pltpu.make_async_copy(kv_hbm.at[g, t - 1], kv_v.at[g], load_sem.at[g])

    def load_own(g):
        return pltpu.make_async_copy(kv_own.at[g], kv_v.at[1 - g], load_sem.at[1 - g])

    def load_sum(g, t):
        return pltpu.make_async_copy(dkv_hbm.at[g, t - 1], tmp, tmp_sem)

    def store_own(g):
        return pltpu.make_async_copy(tmp, own_hbm.at[g], own_sem)

    def load_q(h):
        return pltpu.make_async_copy(q_hbm.at[h], q_v.at[h], in_sem.at[0, h])

    def load_do(h):
        return pltpu.make_async_copy(do_hbm.at[h], do_v.at[h], in_sem.at[1, h])

    def store_dq(h):
        return pltpu.make_async_copy(q_v.at[h], dq_hbm.at[h], out_sem.at[h])

    def terms(h, sums, kv):
        sub = lax.broadcasted_iota(jnp.int32, (LANES, SUB), 0) - h * (2 * PARTS)
        ones_l = jnp.where((sub >= 0) & (sub < PARTS), -1.0, 0.0).astype(BF16)
        ones_d = jnp.where((sub >= PARTS) & (sub < 2 * PARTS), -1.0, 0.0).astype(BF16)

        def probs(qo, ko, width, row, masked):
            qs = pl.ds(qo + row, SUB)
            ks = pl.ds(ko, width)
            stat = stat_v[qs, :]
            wide_l = jnp.concatenate([ones_l] * (width // SUB), axis=1)
            wide_d = jnp.concatenate([ones_d] * (width // SUB), axis=1)
            s = dot_nn(jnp.concatenate([q_v[h, qs, :], stat], axis=1), jnp.concatenate([kv[0:d, ks], wide_l], axis=0))
            p = jnp.exp2(s * factor)
            if masked:
                shape = (SUB, width)
                keep = lax.broadcasted_iota(jnp.int32, shape, 0) + row >= lax.broadcasted_iota(jnp.int32, shape, 1)
                p = jnp.where(keep, p, 0.0)
            dp_ = dot_nn(jnp.concatenate([do_v[h, qs, :], stat], axis=1), jnp.concatenate([kv[d : 2 * d, ks], wide_d], axis=0))
            rows = pl.ds(row, SUB)
            p_scr[rows, 0:width] = p.astype(BF16)
            ds_scr[rows, 0:width] = (p * dp_).astype(BF16)

        def full_unit(qo, ko, fresh=False):
            for row in range(0, half, SUB):
                probs(qo, ko, half, row, False)
            qs = pl.ds(qo, half)
            ks = pl.ds(ko, half)
            p = p_scr[...]
            ds = ds_scr[...]
            sums[d : 2 * d, ks] += dot_nn(dot_v[h, :, qs], p)
            sums[0:d, ks] += dot_nn(qt_v[h, :, qs], ds)
            dq = dot_nt(kv[0:d, ks], ds)
            if fresh:
                dq_v[h, :, qs] = dq
            else:
                dq_v[h, :, qs] += dq

        def diag_unit(off, fresh):
            for row in range(0, half, SUB):
                probs(off, off, row + SUB, row, True)
            for col in range(0, half, SUB):
                qs = pl.ds(off + col, half - col)
                ks = pl.ds(off + col, SUB)
                p = p_scr[pl.ds(col, half - col), pl.ds(col, SUB)]
                ds = ds_scr[pl.ds(col, half - col), pl.ds(col, SUB)]
                sums[d : 2 * d, ks] += dot_nn(dot_v[h, :, qs], p)
                sums[0:d, ks] += dot_nn(qt_v[h, :, qs], ds)
            for row in range(0, half, SUB):
                ds = ds_scr[pl.ds(row, SUB), 0 : row + SUB]
                dq = dot_nt(kv[0:d, pl.ds(off, row + SUB)], ds)
                if fresh:
                    dq_v[h, :, pl.ds(off + row, SUB)] = dq
                else:
                    dq_v[h, :, pl.ds(off + row, SUB)] += dq

        return full_unit, diag_unit

    def transposed(h):
        qt_v[h] = q_v[h].T
        dot_v[h] = do_v[h].T

    def finish(g):
        def body(i, carry):
            h = g * heads + i
            q_v[h] = (dq_v[h] * scale).astype(BF16).T
            store_dq(h).start()
            return carry
        lax.fori_loop(0, heads, body, 0)

    for g in range(groups):
        send_kv(g, 0).start()
    load_own(0).start()
    stat_copy = pltpu.make_async_copy(stat_hbm, stat_v, stat_sem)
    stat_copy.start()

    def load_head(h, carry):
        load_q(h).start()
        load_do(h).start()
        return carry
    lax.fori_loop(0, groups * heads, load_head, 0)
    tmp[...] = jnp.zeros_like(tmp)
    stat_copy.wait()
    load_own(0).wait()

    def own_first(h, carry):
        load_q(h).wait()
        load_do(h).wait()
        transposed(h)
        full_unit, diag_unit = terms(h, tmp, kv_v.at[1])
        full_unit(half, 0, fresh=True)
        diag_unit(0, True)
        diag_unit(half, False)

        @pl.when(h == heads // 2)
        def _():
            wait_kv(0, 0)
            send_kv(0, 1).start()
            load_kv(0, 1).start()
        return carry
    lax.fori_loop(0, heads, own_first, 0)
    store_own(0).start()

    def ring_step(t, carry):
        for g in range(groups):
            load_kv(g, t).wait()
            sel = source_later(t, g)
            off = pl.multiple_of(sel * half, half)

            @pl.when(t >= 2)
            def _():
                send_dkv(g, t - 1).wait_send()
            acc[g] = jnp.zeros((2 * d, tok), F32)

            if g == 0:
                wait_kv(1, t - 1)

                @pl.when(t < n - 1)
                def _():
                    send_kv(1, t).start()
                load_kv(1, t).start()
            else:
                @pl.when(t < n - 1)
                def _():
                    wait_kv(0, t)
                    load_kv(0, t + 1).start()

                @pl.when(t < n - 2)
                def _():
                    send_kv(0, t + 1).start()

                @pl.when(t == n - 1)
                def _():
                    load_own(1).start()

            def head(i, c):
                h = g * heads + i
                if g == 1:
                    @pl.when(t == 1)
                    def _():
                        load_q(h).wait()
                        load_do(h).wait()
                        transposed(h)
                        dq_v[h] = jnp.zeros((d, tok), F32)
                full_unit, _ = terms(h, acc.at[g], kv_v.at[g])
                full_unit(half, 0)
                full_unit(off, off)

                @pl.when((i == heads - 2) & (t >= 2))
                def _():
                    if g == 0:
                        @pl.when(t == 2)
                        def _():
                            store_own(0).wait()
                    send_dkv(g, t - 1).wait_recv()
                    load_sum(g, t - 1).start()
                return c
            lax.fori_loop(0, heads, head, 0)

            @pl.when(t >= 2)
            def _():
                load_sum(g, t - 1).wait()
                acc[g] += tmp[...]
            send_dkv(g, t).start()
        return carry
    lax.fori_loop(1, n, ring_step, 0)

    finish(0)
    tmp[...] = jnp.zeros_like(tmp)
    load_own(1).wait()

    def own_last(i, carry):
        h = heads + i
        full_unit, diag_unit = terms(h, tmp, kv_v.at[0])
        full_unit(half, 0)
        diag_unit(0, False)
        diag_unit(half, False)
        return carry
    lax.fori_loop(0, heads, own_last, 0)
    store_own(1).start()
    finish(1)

    def sent(t, carry):
        for g in range(groups):
            send_kv(g, t).wait_send()
        return carry
    for g in range(groups):
        send_kv(g, 0).wait_send()
    lax.fori_loop(1, n - 1, sent, 0)
    for g in range(groups):
        send_dkv(g, n - 1).wait_send()
        send_dkv(g, n - 1).wait_recv()
    store_own(1).wait()

    def stored(h, carry):
        store_dq(h).wait()
        return carry
    lax.fori_loop(0, groups * heads, stored, 0)


def ring_grads(q, do, stat, kv, dims):
    n_cy, n_cx, groups, heads, tok, d = dims
    n = n_cy * n_cx
    half = tok // 2
    hbm = pl.BlockSpec(memory_space=pl.ANY)
    dma = pltpu.SemaphoreType.DMA
    all_heads = groups * heads
    vmem = pltpu.VMEM
    return pl.pallas_call(
        functools.partial(ring_kernel, dims),
        in_specs=[hbm] * 4,
        out_specs=[hbm] * 4,
        out_shape=[
            jax.ShapeDtypeStruct((all_heads, tok, d), BF16),
            jax.ShapeDtypeStruct((groups, 2 * d, tok), F32),
            jax.ShapeDtypeStruct((groups, n - 1, 2 * d, tok), BF16),
            jax.ShapeDtypeStruct((groups, n - 1, 2 * d, tok), F32),
        ],
        scratch_shapes=[
            vmem((all_heads, tok, d), BF16), vmem((all_heads, tok, d), BF16),
            vmem((all_heads, d, tok), BF16), vmem((all_heads, d, tok), BF16),
            vmem((tok, LANES), BF16), vmem((all_heads, d, tok), F32),
            vmem((groups, 2 * d, tok), BF16), vmem((groups, 2 * d, tok), F32), vmem((2 * d, tok), F32),
            vmem((half, half), BF16), vmem((half, half), BF16),
            dma((2, all_heads)), dma, dma((all_heads,)), dma((groups,)), dma, dma,
            dma((groups, n - 1)), dma((groups, n - 1)), dma((groups, n - 1)), dma((groups, n - 1)),
        ],
        compiler_params=pltpu.CompilerParams(vmem_limit_bytes=67043328, collective_id=0, has_side_effects=True),
        name="ring_grads",
    )(q, do, stat, kv)


def solution(mesh):
    n_cy, n_cx = mesh.shape["cy"], mesh.shape["cx"]
    row_spec = P(("dp", "cy", "cx"), None, None)
    stat_spec = P(("dp", "cy", "cx"), None)

    def local_grads(query_rows, key_rows, value_rows, out_rows, grad_out, log_sum_exp):
        tok, n_heads, d = query_rows.shape
        groups = key_rows.shape[1]
        heads = n_heads // groups
        scale = 1.0 / math.sqrt(d)
        delta = jnp.sum(grad_out.astype(F32) * out_rows.astype(F32), axis=-1)
        parts = jnp.stack([*split3(log_sum_exp / scale), *split3(delta)], axis=-1).reshape(tok, 2 * PARTS * n_heads)
        stat = jnp.pad(parts, ((0, 0), (0, LANES - 2 * PARTS * n_heads))).astype(BF16)
        kv = jnp.concatenate([key_rows.transpose(1, 2, 0), value_rows.transpose(1, 2, 0)], axis=1)
        dims = (n_cy, n_cx, groups, heads, tok, d)
        dq, own, _, sums = ring_grads(query_rows.transpose(1, 0, 2), grad_out.transpose(1, 0, 2), stat, kv, dims)
        total = sums[:, -1] + own
        grad_key = (total[:, :d] * scale).astype(BF16).transpose(2, 0, 1)
        grad_value = total[:, d:].astype(BF16).transpose(2, 0, 1)
        return dq.transpose(1, 0, 2), grad_key, grad_value

    return jax.shard_map(local_grads, mesh=mesh, in_specs=(row_spec,) * 5 + (stat_spec,), out_specs=(row_spec,) * 3, check_vma=False)
```

time: 2420 us -> 515 us (0.21)
  matrix products: 1550 us -> 0 us
  waiting for transfers between devices: 518 us -> 0 us
  Pallas kernels: 0 us -> 487 us
  other arithmetic: 166 us -> 13.9 us
  local copies, waits for them, and re-layouts: 101 us -> 13.1 us
  loops' own time: 63 us -> 0 us
    dot_general x40 -> x0, matrix products: 1550 us -> none  [the longest x8 466 us: block_grads(): jnp.einsum('qkgd,skd->kqgs', do_blk, v_blk, preferred_element_type=jnp.fl...]
    ppermute x30 -> x0, waiting for transfers between devices: 518 us -> none  [the longest x7 415 us: step_body(): v_cur = lax.ppermute(v_cur, ctx_axes, shift_perm)]
    pallas_call x0 -> x1, Pallas kernels: none -> 487 us  [ring_grads(): pl.pallas_call(functools.partial(ring_kernel, dims), in_specs=[hbm] * 4,...]
    add x22 -> x1, other arithmetic: 142 us -> 4.23 us  [local_grads(): total = sums[:, -1] + own]
    another operation x8 -> x0, loops' own time: 63 us -> none  [the longest x7 55.9 us: step_body(): lax.cond(src_rank < ctx_rank, src_before, src_after, k_cur, v_cur)]
    concatenate x7 -> x0, local copies, waits for them, and re-layouts: 59.7 us -> none  [src_after(): return (jnp.concatenate([zero_pad, dq_part], axis=1), dk_part, dv_part)]
    while x32 -> x0, local copies, waits for them, and re-layouts: 33.9 us -> none
  transfers between devices with their start and end apart: 30 -> 0, of which waited for: 15 -> 0; matrix products, arithmetic and copies ran while one was open for 59% -> 0% of each run, Pallas kernels for 0% -> 0%
where the time goes in v2:
time: 515 us
  Pallas kernels  487 us (95%)
  other arithmetic  13.9 us (3%)
  local copies, waits for them, and re-layouts  13.1 us (3%)
    pallas_call x1, Pallas kernels, ring_grads(): pl.pallas_call(functools.partial(ring_kernel, dims), in_specs=[hbm] * 4,...  487 us
    unnamed x11, local copies, waits for them, and re-layouts  11.5 us

profile of v2, /device:TPU:0, one launch (start us, length us, event | category | flops | bytes accessed | tf_op | source)
XLA Modules:
  0.0 514.7 jit_solution(14111084518892783757)
XLA Ops:
  0.6 0.0 copy-start
  0.6 8.0 %multiply_reduce_fusion = f32[2048,12]{0,1:T(8,128)S(1)} fusion(bf16[2048,12,128]{2,0,1:T(8,128)(2,1)} %param.9, bf16[2048,12,128]{2,0,1:T(8,128)(2,1)} %param.10), kind=kLoop, calls=%fused_computation | loop fusion | flops 12558336 | bytes 12681216 | tf_op jit(solution)/shard_map/reduce_sum | solution.py:338
  8.6 0.0 copy-done
  8.6 0.0 copy-start.1
  8.6 0.0 copy-start.2
  8.8 0.2 copy.14
  9.0 0.1 reshape.34
  9.1 0.3 copy.15
  9.4 0.9 pad.5.stat_hbm
  10.3 0.0 copy-done.1
  10.3 0.8 copy.16
  11.1 0.0 copy-done.2
  11.1 0.8 copy.17
  11.9 1.5 pad_maximum_fusion.kv_own
  13.3 486.9 %ring_grads.1 = (bf16[12,2048,128]{2,1,0:T(8,128)(2,1)}, f32[2,256,2048]{2,1,0:T(8,128)}, bf16[2,7,256,2048]{3,2,1,0:T(8,128)(2,1)}, f32[2,7,256,2048]{3,2,1,0:T(8,128)}) custom-call(bf16[12,2048,128]{2,1,0:T(8,128)(2,1)} %bitcast.40, bf16[12,2048,128]{2,1,0:T(8,128)(2,1)} %bitcast.38, bf16[2048,128]{1,0:T(8,128)(2,1)} %pad.5.stat_hbm, ...), custom_call_target="tpu_custom_call" | custom-call | tf_op jit(solution)/shard_map/ring_grads/pallas_call | solution.py:304
  500.3 4.2 bitcast_add_fusion
  504.5 0.1 fusion.2
  504.6 0.2 fusion.1
  504.8 2.0 copy.18
  506.8 2.0 copy.19
  508.8 5.9 %copy.26 = bf16[2048,12,128]{2,0,1:T(8,128)(2,1)} copy(bf16[2048,12,128]{2,0,1:T(8,128)(2,1)} %bitcast.39) | data formatting | bytes 12582912
  (6 shorter events, 0.1 us)
Async XLA Ops:
  0.6 8.0 %copy-start = (f32[2048,12]{0,1:T(8,128)S(1)}, f32[2048,12]{0,1:T(8,128)}, u32[]{:S(2)}) copy-start(f32[2048,12]{0,1:T(8,128)} %param.11) | copy-start | bytes 294916
  8.6 1.7 copy-start.1
  8.6 2.5 copy-start.2

commit v3 on v2

--- a/solution.py
+++ b/solution.py
@@ -170,18 +170,21 @@
     stat_copy.start()
 
     def load_head(h, carry):
-        load_q(h).start()
-        load_do(h).start()
-        return carry
-    lax.fori_loop(0, groups * heads, load_head, 0)
+        for g in range(groups):
+            load_q(g * heads + h).start()
+            load_do(g * heads + h).start()
+        return carry
+    lax.fori_loop(0, heads, load_head, 0)
     tmp[...] = jnp.zeros_like(tmp)
     stat_copy.wait()
     load_own(0).wait()
 
     def own_first(h, carry):
-        load_q(h).wait()
-        load_do(h).wait()
-        transposed(h)
+        for g in range(groups):
+            load_q(g * heads + h).wait()
+            load_do(g * heads + h).wait()
+            transposed(g * heads + h)
+        dq_v[heads + h] = jnp.zeros((d, tok), F32)
         full_unit, diag_unit = terms(h, tmp, kv_v.at[1])
         full_unit(half, 0, fresh=True)
         diag_unit(0, True)
@@ -230,13 +233,6 @@
 
             def head(i, c):
                 h = g * heads + i
-                if g == 1:
-                    @pl.when(t == 1)
-                    def _():
-                        load_q(h).wait()
-                        load_do(h).wait()
-                        transposed(h)
-                        dq_v[h] = jnp.zeros((d, tok), F32)
                 full_unit, _ = terms(h, acc.at[g], kv_v.at[g])
                 full_unit(half, 0)
                 full_unit(off, off)

time: 515 us -> 514 us (level)
  no operation moved by 1% of the time
where the time goes in v3:
time: 514 us
  Pallas kernels  486 us (95%)
  other arithmetic  13.9 us (3%)
  local copies, waits for them, and re-layouts  13.1 us (3%)
    pallas_call x1, Pallas kernels, ring_grads(): pl.pallas_call(functools.partial(ring_kernel, dims), in_specs=[hbm] * 4,...  486 us
    unnamed x11, local copies, waits for them, and re-layouts  11.5 us

profile of v3, /device:TPU:0, one launch (start us, length us, event | category | flops | bytes accessed | tf_op | source)
XLA Modules:
  0.0 514.3 jit_solution(12907178432587634859)
XLA Ops:
  0.6 0.0 copy-start
  0.6 8.0 %multiply_reduce_fusion = f32[2048,12]{0,1:T(8,128)S(1)} fusion(bf16[2048,12,128]{2,0,1:T(8,128)(2,1)} %param.9, bf16[2048,12,128]{2,0,1:T(8,128)(2,1)} %param.10), kind=kLoop, calls=%fused_computation | loop fusion | flops 12558336 | bytes 12681216 | tf_op jit(solution)/shard_map/reduce_sum | solution.py:334
  8.6 0.0 copy-done
  8.6 0.0 copy-start.1
  8.6 0.0 copy-start.2
  8.8 0.2 copy.14
  9.0 0.1 reshape.34
  9.1 0.3 copy.15
  9.4 0.9 pad.5.stat_hbm
  10.3 0.0 copy-done.1
  10.3 0.8 copy.16
  11.1 0.0 copy-done.2
  11.1 0.8 copy.17
  11.9 1.5 pad_maximum_fusion.kv_own
  13.3 486.5 %ring_grads.1 = (bf16[12,2048,128]{2,1,0:T(8,128)(2,1)}, f32[2,256,2048]{2,1,0:T(8,128)}, bf16[2,7,256,2048]{3,2,1,0:T(8,128)(2,1)}, f32[2,7,256,2048]{3,2,1,0:T(8,128)}) custom-call(bf16[12,2048,128]{2,1,0:T(8,128)(2,1)} %bitcast.40, bf16[12,2048,128]{2,1,0:T(8,128)(2,1)} %bitcast.38, bf16[2048,128]{1,0:T(8,128)(2,1)} %pad.5.stat_hbm, ...), custom_call_target="tpu_custom_call" | custom-call | tf_op jit(solution)/shard_map/ring_grads/pallas_call | solution.py:300
  499.8 4.2 bitcast_add_fusion
  504.0 0.1 fusion.2
  504.2 0.2 fusion.1
  504.4 2.0 copy.18
  506.4 2.0 copy.19
  508.4 5.9 %copy.26 = bf16[2048,12,128]{2,0,1:T(8,128)(2,1)} copy(bf16[2048,12,128]{2,0,1:T(8,128)(2,1)} %bitcast.39) | data formatting | bytes 12582912
  (6 shorter events, 0.1 us)
Async XLA Ops:
  0.6 8.0 %copy-start = (f32[2048,12]{0,1:T(8,128)S(1)}, f32[2048,12]{0,1:T(8,128)}, u32[]{:S(2)}) copy-start(f32[2048,12]{0,1:T(8,128)} %param.11) | copy-start | bytes 294916
  8.6 1.7 copy-start.1
  8.6 2.5 copy-start.2
